TPU v7x, 128 devices: a whole 4x4x4 slice. The times are simulated.
128 devices in a mesh: rep: 16 (over y_hi, z, core), tp: 8 (over y_lo, x).
Axes of the slice: x: 4, y: 4 (y_hi: 2, y_lo: 2; y = y_hi * 2 + y_lo), z: 4, core: 2. Of those that a mesh axis runs over, the one named last changes fastest.
Arguments:
- delta_query: bfloat16 [16, 2, 2048, 3072], P('rep', None, None, 'tp'), may hold values from -6 to 6
- master_query: float32 [2, 2048, 3072], P(None, 'rep', 'tp'), may hold values from -3 to 3
- moment_query: float32 [2, 2048, 3072], P(None, 'rep', 'tp'), may hold values from -3 to 3
- delta_latent: bfloat16 [16, 2, 512, 4096], P('rep', None, None, 'tp'), may hold values from -6 to 6
- master_latent: float32 [2, 512, 4096], P(None, 'rep', 'tp'), may hold values from -3 to 3
- moment_latent: float32 [2, 512, 4096], P(None, 'rep', 'tp'), may hold values from -3 to 3
- delta_output: bfloat16 [16, 2, 2048, 2048], P('rep', None, 'tp'), may hold values from -6 to 6
- master_output: float32 [2, 2048, 2048], P(None, 'tp', 'rep'), may hold values from -3 to 3
- moment_output: float32 [2, 2048, 2048], P(None, 'tp', 'rep'), may hold values from -3 to 3
Outputs:
- params_query: bfloat16 [2, 2048, 3072], P(None, None, 'tp')
- new_master_query: float32 [2, 2048, 3072], P(None, 'rep', 'tp')
- new_moment_query: float32 [2, 2048, 3072], P(None, 'rep', 'tp')
- params_latent: bfloat16 [2, 512, 4096], P(None, None, 'tp')
- new_master_latent: float32 [2, 512, 4096], P(None, 'rep', 'tp')
- new_moment_latent: float32 [2, 512, 4096], P(None, 'rep', 'tp')
- params_output: bfloat16 [2, 2048, 2048], P(None, 'tp')
- new_master_output: float32 [2, 2048, 2048], P(None, 'tp', 'rep')
- new_moment_output: float32 [2, 2048, 2048], P(None, 'tp', 'rep')
All inputs are finite; a program needn't handle non-finite values.
Results may differ from a plain program's by a relative error of at most 0.012.
Values may be sent and summed in bfloat16 or wider, within the bound.
A program may use at most 64 MiB of HBM per device.

v0:
```python
import jax
import jax.numpy as jnp
from jax import lax
from jax.sharding import Mesh
from jax.sharding import PartitionSpec as P

REP = ("rep_0", "rep_1", "rep_2")


OUTER_RATE = 0.7
OUTER_MOMENTUM = 0.9


def in_blocks(value, dim, length):
    lengths = value.shape
    blocks = value.reshape(*lengths[:dim], length, lengths[dim] // length, *lengths[dim + 1 :])
    return jnp.moveaxis(blocks, dim, 0)


def joined_along(blocks, dim):
    lengths = list(blocks.shape[1:])
    lengths[dim] *= blocks.shape[0]
    return jnp.moveaxis(blocks, 0, dim).reshape(lengths)


def moved_by_axis(blocks, axes, order):
    inside = blocks.shape[1:]
    out = blocks.reshape(*(lax.axis_size(a) for a in axes), *inside)
    for k in order:
        out = lax.all_to_all(out, axes[k], k, k, tiled=True)
    return out.reshape(-1, *inside)


def core_and_chips(value, groups, order, split_dim, concat_dim):
    length = lax.axis_size(groups[0]) * lax.axis_size(groups[1])
    blocks = in_blocks(value, split_dim, length)
    return joined_along(moved_by_axis(blocks, groups, order), concat_dim)


def copy_for_each(value, axis):
    length = lax.axis_size(axis)
    return lax.all_to_all(
        jnp.broadcast_to(value[None], (length, *value.shape)), axis, 0, 0, tiled=True
    )


def gathered_copies(value, axis, dim):
    blocks = copy_for_each(value, axis)
    return joined_along(blocks, dim)


def nesterov(totals, master, moment, replica_count):
    average = totals / replica_count
    momentum = OUTER_MOMENTUM * moment + average
    updated = master - OUTER_RATE * (average + OUTER_MOMENTUM * momentum)
    return (updated, momentum)


def outer_step(
    delta_query,
    master_query,
    moment_query,
    delta_latent,
    master_latent,
    moment_latent,
    delta_output,
    master_output,
    moment_output,
):
    replica_count = lax.axis_size(REP)
    query_terms = core_and_chips(delta_query, (("rep_0", "rep_1"), "rep_2"), (1, 0), 2, 0)
    latent_terms = lax.all_to_all(delta_latent, REP, split_axis=2, concat_axis=0, tiled=True)
    output_terms = lax.all_to_all(delta_output, REP, split_axis=3, concat_axis=0, tiled=True)
    query_totals = jnp.sum(query_terms.astype(jnp.float32), 0)
    latent_totals = jnp.sum(latent_terms.astype(jnp.float32), 0)
    output_totals = jnp.sum(output_terms.astype(jnp.float32), 0)
    query_master, query_moment = nesterov(query_totals, master_query, moment_query, replica_count)
    latent_master, latent_moment = nesterov(
        latent_totals, master_latent, moment_latent, replica_count
    )
    output_master, output_moment = nesterov(
        output_totals, master_output, moment_output, replica_count
    )
    query_params = lax.all_gather(query_master.astype(jnp.bfloat16), REP, axis=1, tiled=True)
    latent_params = gathered_copies(latent_master.astype(jnp.bfloat16), REP, 1)
    output_params = lax.all_gather(output_master.astype(jnp.bfloat16), REP, axis=2, tiled=True)
    return (
        query_params,
        query_master,
        query_moment,
        latent_params,
        latent_master,
        latent_moment,
        output_params,
        output_master,
        output_moment,
    )


def on_device(
    delta_query,
    master_query,
    moment_query,
    delta_latent,
    master_latent,
    moment_latent,
    delta_output,
    master_output,
    moment_output,
):
    return outer_step(
        delta_query,
        master_query,
        moment_query,
        delta_latent,
        master_latent,
        moment_latent,
        delta_output,
        master_output,
        moment_output,
    )


def solution(mesh):
    torus = Mesh(mesh.devices.reshape(2, 4, 2, mesh.shape["tp"]), ("rep_0", "rep_1", "rep_2", "tp"))
    return jax.shard_map(
        on_device,
        mesh=torus,
        in_specs=(
            P(REP, None, None, "tp"),
            P(None, REP, "tp"),
            P(None, REP, "tp"),
            P(REP, None, None, "tp"),
            P(None, REP, "tp"),
            P(None, REP, "tp"),
            P(REP, None, "tp", None),
            P(None, "tp", REP),
            P(None, "tp", REP),
        ),
        out_specs=(
            P(None, None, "tp"),
            P(None, REP, "tp"),
            P(None, REP, "tp"),
            P(None, None, "tp"),
            P(None, REP, "tp"),
            P(None, REP, "tp"),
            P(None, "tp", None),
            P(None, "tp", REP),
            P(None, "tp", REP),
        ),
        check_vma=False,
    )
```

profile of v0, /device:TPU:1, one launch (start us, length us, event | category | flops | bytes accessed | tf_op | source)
XLA Modules:
  0.0 191.4 jit_solution(4195767868516132089)
XLA Ops:
  7.2 6.2 %copy.70 = bf16[1,2,256,2048]{2,1,0,3:T(2,128)(2,1)} copy(bf16[1,2,256,2048]{3,2,1,0:T(8,128)(2,1)} %param.15) | data formatting | bytes 4194304 | tf_op args[6]
  13.4 9.6 %all-to-all-start.4 = ((bf16[1,2,256,2048]{2,1,0,3:T(2,128)(2,1)}), bf16[1,2,256,2048]{2,1,0,3:T(2,128)(2,1)S(1)}, u32[]{:S(2)}, u32[]{:S(2)}) async-start(bf16[1,2,256,2048]{2,1,0,3:T(2,128)(2,1)} %copy.70), calls=%async_computation.4 | async-start | bytes 4194304 | tf_op jit(solution)/shard_map/all_to_all | solution.py:73
  23.3 28.0 %all-to-all-done.4 = bf16[1,2,256,2048]{2,1,0,3:T(2,128)(2,1)S(1)} async-done(((bf16[1,2,256,2048]{2,1,0,3:T(2,128)(2,1)}), bf16[1,2,256,2048]{2,1,0,3:T(2,128)(2,1)S(1)}, u32[]{:S(2)}, u32[]{:S(2)}) %all-to-all-start.4) | async-done | bytes 2097184 | tf_op jit(solution)/shard_map/all_to_all | solution.py:73
  51.3 1.8 convert_reduce_fusion.1
  53.1 1.1 fusion
  54.2 2.4 %copy.65 = bf16[8,2,1,2,128,384]{5,4,0,3,2,1:T(8,128)(2,1)S(1)} copy(bf16[8,2,1,2,128,384]{5,4,1,0,3,2:T(8,128)(2,1)} %bitcast.14) | data formatting | bytes 6291456 | tf_op jit(solution)/shard_map/reshape | solution.py:28
  56.6 6.9 %all_to_all.33 = bf16[8,2,1,2,128,384]{5,4,0,3,2,1:T(8,128)(2,1)S(1)} all-to-all(bf16[8,2,1,2,128,384]{5,4,0,3,2,1:T(8,128)(2,1)S(1)} %copy.65), channel_id=1, replica_groups=mesh['rep_0'=2,'rep_1'=4,'rep_2'=2,'tp'=8] {'rep_2'}, dimensions={1} | all-to-all | bytes 6291456 | tf_op jit(solution)/shard_map/all_to_all | solution.py:30
  63.6 0.5 copy.66
  64.1 49.1 %all_to_all.34 = bf16[8,2,1,2,128,384]{5,4,1,3,2,0:T(8,128)(2,1)S(1)} all-to-all(bf16[8,2,1,2,128,384]{5,4,1,3,2,0:T(8,128)(2,1)S(1)} %copy.66), channel_id=1, replica_groups=mesh['rep_0'=2,'rep_1'=4,'rep_2'=2,'tp'=8] {'rep_0','rep_1'}, dimensions={0} | all-to-all | bytes 6291456 | tf_op jit(solution)/shard_map/all_to_all | solution.py:30
  113.2 0.4 convert_reduce_fusion
  113.7 0.6 copy-done.1
  114.3 1.0 fusion.2
  115.4 1.1 copy.67
  116.5 23.9 %all_to_all.35 = bf16[1,2,512,512]{3,1,0,2:T(2,128)(2,1)S(1)} all-to-all(bf16[1,2,512,512]{3,1,0,2:T(2,128)(2,1)S(1)} %copy.67), channel_id=1, replica_groups=mesh['rep_0'=2,'rep_1'=4,'rep_2'=2,'tp'=8] {'rep_0','rep_1','rep_2'}, dimensions={2} | all-to-all | bytes 2097152 | tf_op jit(solution)/shard_map/all_to_all | solution.py:72
  140.4 0.9 convert_reduce_fusion.2
  141.3 0.8 fusion.1
  142.0 1.1 broadcast_in_dim.2
  143.1 4.7 %all-to-all-start.3 = ((bf16[16,2,32,512]{3,2,1,0:T(8,128)(2,1)}), bf16[16,2,32,512]{3,2,1,0:T(8,128)(2,1)S(1)}, u32[]{:S(2)}, u32[]{:S(2)}) async-start(bf16[16,2,32,512]{3,2,1,0:T(8,128)(2,1)} %broadcast_in_dim.2), calls=%async_computation.3 | async-start | bytes 2097152 | tf_op jit(solution)/shard_map/all_to_all | solution.py:42
  147.8 0.8 copy.74
  148.7 0.8 copy.75
  149.5 23.9 %all-to-all-done.3 = bf16[16,2,32,512]{3,2,1,0:T(8,128)(2,1)S(1)} async-done(((bf16[16,2,32,512]{3,2,1,0:T(8,128)(2,1)}), bf16[16,2,32,512]{3,2,1,0:T(8,128)(2,1)S(1)}, u32[]{:S(2)}, u32[]{:S(2)}) %all-to-all-start.3) | async-done | bytes 1048608 | tf_op jit(solution)/shard_map/all_to_all | solution.py:42
  173.4 1.0 copy.69
  174.5 6.2 %copy.73 = bf16[2,256,2048]{2,1,0:T(8,128)(2,1)} copy(bf16[2,256,2048]{1,0,2:T(2,128)(2,1)} %all-gather.5.cloned.1.call-done) | data formatting | bytes 4194304
  180.7 3.9 %copy.86 = bf16[2,2048,384]{2,1,0:T(8,128)(2,1)} copy(bf16[2,2048,384]{2,1,0:T(8,128)(2,1)} %all-gather.3.cloned.1.call-done) | data formatting | bytes 6291456
  (21 shorter events, 0.5 us)
Async XLA Ops:
  7.2 15.8 %copy-start.3 = (f32[2,256,128]{2,1,0:T(8,128)S(1)}, f32[2,256,128]{2,1,0:T(8,128)}, u32[]{:S(2)}) copy-start(f32[2,256,128]{2,1,0:T(8,128)} %param.17) | copy-start | bytes 786436
  13.4 9.8 %copy-start.4 = (f32[2,256,128]{2,1,0:T(8,128)S(1)}, f32[2,256,128]{2,1,0:T(8,128)}, u32[]{:S(2)}) copy-start(f32[2,256,128]{2,1,0:T(8,128)} %param.16) | copy-start | bytes 786436
  13.4 37.9 %all-to-all-start.4 = ((bf16[1,2,256,2048]{2,1,0,3:T(2,128)(2,1)}), bf16[1,2,256,2048]{2,1,0,3:T(2,128)(2,1)S(1)}, u32[]{:S(2)}, u32[]{:S(2)}) async-start(bf16[1,2,256,2048]{2,1,0,3:T(2,128)(2,1)} %copy.70), calls=%async_computation.4 | async-start | bytes 4194304 | tf_op jit(solution)/shard_map/all_to_all | solution.py:73
  23.0 151.5 %all-gather.5.cloned.1.call-start = ((), (), s32[]{:S(2)}) async-start(), calls=%async_computation.6 | async-start | bytes 2228224 | tf_op jit(solution)/shard_map/all_gather | solution.py:86
  54.2 126.5 %all-gather.3.cloned.1.call-start = ((), (), s32[]{:S(2)}) async-start(), calls=%async_computation.5 | async-start | bytes 3342336 | tf_op jit(solution)/shard_map/all_gather | solution.py:84
  113.2 1.0 copy-start.1
  113.2 1.1 copy-start.2
  113.2 2.2 %copy-start = (bf16[1,2,512,512]{3,2,1,0:T(8,128)(2,1)S(1)}, bf16[1,2,512,512]{3,2,1,0:T(8,128)(2,1)}, u32[]{:S(2)}) copy-start(bf16[1,2,512,512]{3,2,1,0:T(8,128)(2,1)} %param.12) | copy-start | bytes 3145732
  115.4 25.9 %copy-start.5 = (f32[2,32,512]{2,1,0:T(8,128)S(1)}, f32[2,32,512]{2,1,0:T(8,128)}, u32[]{:S(2)}) copy-start(f32[2,32,512]{2,1,0:T(8,128)} %param.13) | copy-start | bytes 393220
  115.4 25.9 %copy-start.6 = (f32[2,32,512]{2,1,0:T(8,128)S(1)}, f32[2,32,512]{2,1,0:T(8,128)}, u32[]{:S(2)}) copy-start(f32[2,32,512]{2,1,0:T(8,128)} %param.14) | copy-start | bytes 393220
  143.1 30.3 %all-to-all-start.3 = ((bf16[16,2,32,512]{3,2,1,0:T(8,128)(2,1)}), bf16[16,2,32,512]{3,2,1,0:T(8,128)(2,1)S(1)}, u32[]{:S(2)}, u32[]{:S(2)}) async-start(bf16[16,2,32,512]{3,2,1,0:T(8,128)(2,1)} %broadcast_in_dim.2), calls=%async_computation.3 | async-start | bytes 2097152 | tf_op jit(solution)/shard_map/all_to_all | solution.py:42
Sparse Core Ops, SparseCore 0:
  54.3 58.2 all-gather.4
  115.7 63.2 all-gather.2
where the time goes:
time: 192 us; the launch traced here: 191 us
  blocking collectives  79.9 us (42%)
  waiting for transfers between devices  51.9 us (27%)
  local copies, waits for them, and re-layouts  25 us (13%)
  starting transfers between devices  14.4 us (8%)
  between operations  14.2 us (7%)
  other arithmetic  5.96 us (3%)
    all_to_all x2, blocking collectives, moved_by_axis(): out = lax.all_to_all(out, axes[k], k, k, tiled=True)  56.1 us
    all_to_all x1, waiting for transfers between devices, outer_step(): lax.all_to_all(delta_output, REP, split_axis=3, concat_axis=0, tiled=True)  28 us
    all_to_all x1, waiting for transfers between devices, copy_for_each(): lax.all_to_all(jnp.broadcast_to(value[None], (length, *value.shape)), axi...  23.9 us
    all_to_all x1, blocking collectives, outer_step(): lax.all_to_all(delta_latent, REP, split_axis=2, concat_axis=0, tiled=True)  23.9 us
    unnamed x22, local copies, waits for them, and re-layouts  20 us
    all_to_all x1, starting transfers between devices, outer_step(): lax.all_to_all(delta_output, REP, split_axis=3, concat_axis=0, tiled=True)  9.58 us
    all_to_all x1, starting transfers between devices, copy_for_each(): lax.all_to_all(jnp.broadcast_to(value[None], (length, *value.shape)), axi...  4.7 us
  transfers between devices with their start and end apart: 4, of which 2 were waited for; matrix products, arithmetic and copies ran while one was open for 9% of the time, Pallas kernels for 0%

commit v1 on v0

v1 whole, which is shorter than its diff:
```python
import jax
import jax.numpy as jnp
from jax import lax
from jax.experimental import pallas as pl
from jax.experimental.pallas import tpu as pltpu
from jax.sharding import Mesh
from jax.sharding import PartitionSpec as P

REP = ("yh", "z", "c")
TP = ("yl", "x")
MESH = pl.DeviceIdType.MESH

OUTER_RATE = 0.7
OUTER_MOMENTUM = 0.9
REPLICAS = 16

BLOCKS = ((128, 384), (32, 512), (256, 128))
LAYERS = 2
Z_FIRST = ((0, 0), (0, 1))
Y_FIRST = ((1, 0), (1, 1), (2, 0), (2, 1))
COPIES = 256
LOADS = 64


def outer_kernel(*refs):
    f32, bf16 = jnp.float32, jnp.bfloat16
    delta, master, moment = refs[0:9:3], refs[1:9:3], refs[2:9:3]
    params, new_master, new_moment = refs[9:18:3], refs[10:18:3], refs[11:18:3]
    own, peer, far, direct, summed, across, held_master, held_moment = (
        refs[18 + 3 * i : 21 + 3 * i] for i in range(8)
    )
    load_sem, send_sem, recv_sem = refs[42:]

    yh, z, c = (lax.axis_index(a) for a in REP)
    zs = [lax.rem(z + k, 4) for k in range(4)]
    ys = [yh, 1 - yh]
    core_to, y_to = {"c": 1 - c}, {"yh": 1 - yh}

    def up(layer):
        return 1 if layer == 0 else 3

    def down(layer):
        return 3 if layer == 0 else 1

    started, loads = [], []

    def send(src, dst, to):
        i = len(started)
        copy = pltpu.make_async_remote_copy(
            src_ref=src,
            dst_ref=dst,
            send_sem=send_sem.at[i],
            recv_sem=recv_sem.at[i],
            device_id=to,
            device_id_type=MESH,
        )
        copy.start()
        started.append(copy)
        return copy

    def load(src, dst):
        copy = pltpu.make_async_copy(src, dst, load_sem.at[len(loads)])
        copy.start()
        loads.append(copy)
        return copy

    def block(ref, a, layer, y, zz, core):
        if a < 2:
            return ref[a].at[layer, y, zz, core]
        column = pl.multiple_of(((y * 4 + zz) * 2 + core) * 128, 128)
        return ref[2].at[layer, :, pl.ds(column, 128)]

    order = [(a, l, 2, j) for a, l in Z_FIRST for j in (0, 1)]
    order += [(a, l, 2, 1) for a, l in Y_FIRST]
    order += [(a, l, down(l), j) for a, l in Z_FIRST for j in (0, 1)]
    order += [(a, l, k, 1) for k in (1, 3) for a, l in Y_FIRST]
    order += [(a, l, up(l), j) for a, l in Z_FIRST for j in (0, 1)]
    order += [(a, l, 0, 1) for a, l in Y_FIRST]
    order += [(a, l, 2, 0) for a, l in Y_FIRST]
    order += [(a, l, k, 0) for k in (1, 3) for a, l in Y_FIRST]
    order += [(a, l, 0, j) for a, l in Z_FIRST for j in (0, 1)]
    order += [(a, l, 0, 0) for a, l in Y_FIRST]

    loaded, from_peer = {}, {}
    for a, l, k, j in order:
        loaded[a, l, k, j] = load(block(delta, a, l, ys[j], zs[k], c), own[a].at[l, k, j])
    state = []
    for a in range(3):
        state.append(load(master[a], held_master[a]))
        state.append(load(moment[a], held_moment[a]))

    barrier = pltpu.get_barrier_semaphore()
    for to in (core_to, {"z": zs[1]}, {"z": zs[3]}, y_to):
        pl.semaphore_signal(barrier, inc=1, device_id=to, device_id_type=MESH)
    pl.semaphore_wait(barrier, 4)

    for a, l, k, j in order:
        from_peer[a, l, k, j] = send(
            block(delta, a, l, ys[j], zs[k], 1 - c), peer[a].at[l, k, j], core_to
        )

    def pair(a, l, k, j):
        loaded[a, l, k, j].wait()
        from_peer[a, l, k, j].wait_recv()
        own[a][l, k, j] = own[a][l, k, j] + peer[a][l, k, j]

    got = {}
    for a, l in Z_FIRST:
        pair(a, l, 2, 0)
        pair(a, l, 2, 1)
    for a, l in Z_FIRST:
        got["far", a, l] = send(own[a].at[l, 2], far[a].at[l], {"z": zs[up(l)]})
    for a, l in Y_FIRST:
        pair(a, l, 2, 1)
    for a, l in Y_FIRST:
        got["y", a, l, 2] = send(own[a].at[l, 2, 1], across[a].at[l, 2], y_to)
    for a, l in Z_FIRST:
        pair(a, l, down(l), 0)
        pair(a, l, down(l), 1)
    for a, l in Z_FIRST:
        got["direct", a, l] = send(own[a].at[l, down(l)], direct[a].at[l], {"z": zs[down(l)]})
    for k in (1, 3):
        for a, l in Y_FIRST:
            pair(a, l, k, 1)
        for a, l in Y_FIRST:
            got["y", a, l, k] = send(own[a].at[l, k, 1], across[a].at[l, k], y_to)
    for a, l in Z_FIRST:
        pair(a, l, up(l), 0)
        pair(a, l, up(l), 1)
    for a, l in Y_FIRST:
        pair(a, l, 0, 1)
    for a, l in Y_FIRST:
        got["y", a, l, 0] = send(own[a].at[l, 0, 1], across[a].at[l, 0], y_to)
    for k in (2, 1, 3):
        for a, l in Y_FIRST:
            pair(a, l, k, 0)
    for a, l in Z_FIRST:
        pair(a, l, 0, 0)
        pair(a, l, 0, 1)
    for a, l in Y_FIRST:
        pair(a, l, 0, 0)

    for a, l in Z_FIRST:
        got["far", a, l].wait_recv()
        own[a][l, up(l)] = (
            own[a][l, up(l)].astype(f32) + far[a][l].astype(f32)
        ).astype(bf16)
        got["summed", a, l] = send(own[a].at[l, up(l)], summed[a].at[l], {"z": zs[up(l)]})
    for a, l in Y_FIRST:
        got["y", a, l, 2].wait_recv()
        own[a][l, 2, 0] = own[a][l, 2, 0] + across[a][l, 2]
        got["far", a, l] = send(own[a].at[l, 2, 0], far[a].at[l, 0], {"z": zs[up(l)]})
    for k in (1, 3):
        for a, l in Y_FIRST:
            got["y", a, l, k].wait_recv()
            if k == down(l):
                own[a][l, k, 0] = own[a][l, k, 0] + across[a][l, k]
                got["direct", a, l] = send(
                    own[a].at[l, k, 0], direct[a].at[l, 0], {"z": zs[k]}
                )
    total = {}
    for a, l in Z_FIRST:
        got["direct", a, l].wait_recv()
        got["summed", a, l].wait_recv()
        mine = [
            own[a][l, 0, j].astype(f32) + direct[a][l, j].astype(f32) + summed[a][l, j].astype(f32)
            for j in (0, 1)
        ]
        own[a][l, 0, 1] = mine[1].astype(bf16)
        got["y", a, l, 0] = send(own[a].at[l, 0, 1], across[a].at[l, 0], y_to)
    for a, l in Y_FIRST:
        got["far", a, l].wait_recv()
        k = up(l)
        own[a][l, k, 0] = (
            own[a][l, k, 0].astype(f32)
            + across[a][l, k].astype(f32)
            + far[a][l, 0].astype(f32)
        ).astype(bf16)
        got["summed", a, l] = send(own[a].at[l, k, 0], summed[a].at[l, 0], {"z": zs[k]})

    for copy in state:
        copy.wait()

    def update(a, l):
        pieces = [own[a][l, 0, 0], direct[a][l, 0], summed[a][l, 0], across[a][l, 0]]
        average = sum(piece.astype(f32) for piece in pieces) * (1.0 / REPLICAS)
        momentum = OUTER_MOMENTUM * held_moment[a][l] + average
        updated = held_master[a][l] - OUTER_RATE * (average + OUTER_MOMENTUM * momentum)
        new_moment[a][l] = momentum
        new_master[a][l] = updated
        block(params, a, l, yh, z, c)[...] = updated.astype(bf16)

    def share(a, l, y, zz, to):
        piece = block(params, a, l, y, zz, c)
        return send(piece, piece, to)

    to_core = []

    def core_share(a, l, y, k):
        to_core.append(share(a, l, y, zs[k], core_to))

    for a, l in Y_FIRST:
        got["y", a, l, 0].wait_recv()
        got["direct", a, l].wait_recv()
        got["summed", a, l].wait_recv()
        update(a, l)
    up_copy, down_copy, on_copy, y_copy = {}, {}, {}, {}

    def z_share(a, l, j):
        up_copy[a, l, j] = share(a, l, ys[j], z, {"z": zs[up(l)]})

    def z_share_back(a, l, j):
        down_copy[a, l, j] = share(a, l, ys[j], z, {"z": zs[down(l)]})

    for a, l in Y_FIRST:
        z_share(a, l, 0)
    for a, l in Y_FIRST:
        y_copy[a, l, 0] = share(a, l, yh, z, y_to)
    for a, l in Y_FIRST:
        z_share_back(a, l, 0)
    for a, l in Y_FIRST:
        core_share(a, l, yh, 0)

    for a, l in Z_FIRST:
        got["y", a, l, 0].wait_recv()
        update(a, l)
    for a, l in Z_FIRST:
        y_copy[a, l, 0] = share(a, l, yh, z, y_to)
    for a, l in Z_FIRST:
        core_share(a, l, yh, 0)
    for a, l in Y_FIRST:
        up_copy[a, l, 0].wait_recv()
        on_copy[a, l, 0] = share(a, l, yh, zs[down(l)], {"z": zs[up(l)]})
    for a, l in Z_FIRST:
        z_share(a, l, 0)
    for a, l in Z_FIRST:
        z_share_back(a, l, 0)
    for a, l in Y_FIRST:
        y_copy[a, l, down(l)] = share(a, l, yh, zs[down(l)], y_to)
        core_share(a, l, yh, down(l))
    for a, l in Y_FIRST:
        down_copy[a, l, 0].wait_recv()
        y_copy[a, l, up(l)] = share(a, l, yh, zs[up(l)], y_to)
        core_share(a, l, yh, up(l))
    for a, l in Y_FIRST:
        on_copy[a, l, 0].wait_recv()
        y_copy[a, l, 2] = share(a, l, yh, zs[2], y_to)
        core_share(a, l, yh, 2)
    for a, l in Y_FIRST:
        y_copy[a, l, 0].wait_recv()
        core_share(a, l, ys[1], 0)
    for a, l in Z_FIRST:
        y_copy[a, l, 0].wait_recv()
        z_share(a, l, 1)
    for a, l in Z_FIRST:
        up_copy[a, l, 0].wait_recv()
        on_copy[a, l, 0] = share(a, l, yh, zs[down(l)], {"z": zs[up(l)]})
    for a, l in Z_FIRST:
        z_share_back(a, l, 1)
        core_share(a, l, ys[1], 0)
        core_share(a, l, yh, down(l))
    for a, l in Z_FIRST:
        down_copy[a, l, 0].wait_recv()
        core_share(a, l, yh, up(l))
    for k in (1, 3):
        for a, l in Y_FIRST:
            if k == down(l):
                y_copy[a, l, k].wait_recv()
                core_share(a, l, ys[1], k)
    for a, l in Z_FIRST:
        on_copy[a, l, 0].wait_recv()
        core_share(a, l, yh, 2)
    for a, l in Z_FIRST:
        up_copy[a, l, 1].wait_recv()
        on_copy[a, l, 1] = share(a, l, ys[1], zs[down(l)], {"z": zs[up(l)]})
        core_share(a, l, ys[1], down(l))
    for a, l in Z_FIRST:
        down_copy[a, l, 1].wait_recv()
        core_share(a, l, ys[1], up(l))
    for k in (1, 3):
        for a, l in Y_FIRST:
            if k == up(l):
                y_copy[a, l, k].wait_recv()
                core_share(a, l, ys[1], k)
    for a, l in Z_FIRST:
        on_copy[a, l, 1].wait_recv()
        core_share(a, l, ys[1], 2)
    for a, l in Y_FIRST:
        y_copy[a, l, 2].wait_recv()
        core_share(a, l, ys[1], 2)
    for copy in to_core:
        copy.wait_recv()
    for copy in started:
        copy.wait_send()


def outer_step(
    delta_query,
    master_query,
    moment_query,
    delta_latent,
    master_latent,
    moment_latent,
    delta_output,
    master_output,
    moment_output,
):
    f32, bf16 = jnp.float32, jnp.bfloat16
    shapes = []
    for a, block in enumerate(BLOCKS):
        whole = (LAYERS, 2, 4, 2, *block) if a < 2 else (LAYERS, block[0], 16 * block[1])
        shapes += [(whole, bf16), ((LAYERS, *block), f32), ((LAYERS, *block), f32)]
    pieces = [(LAYERS, 4, 2), (LAYERS, 4, 2), (LAYERS, 2), (LAYERS, 2), (LAYERS, 2), (LAYERS, 4)]
    scratch = [pltpu.VMEM((*lead, *block), bf16) for lead in pieces for block in BLOCKS]
    scratch += [pltpu.VMEM((LAYERS, *block), f32) for _ in range(2) for block in BLOCKS]
    results = pl.pallas_call(
        outer_kernel,
        out_shape=tuple(pltpu.VMEM(*shape) for shape in shapes),
        in_specs=[pl.BlockSpec(memory_space=pl.ANY)] * 9,
        out_specs=tuple(pl.BlockSpec(memory_space=pltpu.VMEM) for _ in range(9)),
        scratch_shapes=scratch
        + [
            pltpu.SemaphoreType.DMA((LOADS,)),
            pltpu.SemaphoreType.DMA((COPIES,)),
            pltpu.SemaphoreType.DMA((COPIES,)),
        ],
        compiler_params=pltpu.CompilerParams(
            collective_id=0, has_side_effects=True, vmem_limit_bytes=40 * 1024 * 1024
        ),
    )(
        delta_query.reshape(shapes[0][0]),
        master_query,
        moment_query,
        delta_latent.reshape(shapes[3][0]),
        master_latent,
        moment_latent,
        delta_output.reshape(shapes[6][0]),
        master_output,
        moment_output,
    )
    query, latent = results[0], results[3]
    return (
        query.reshape(LAYERS, 2048, 384),
        *results[1:3],
        latent.reshape(LAYERS, 512, 512),
        *results[4:],
    )


def solution(mesh):
    torus = Mesh(mesh.devices.reshape(2, 4, 2, 2, 4), (*REP, *TP))
    return jax.shard_map(
        outer_step,
        mesh=torus,
        in_specs=(
            P(REP, None, None, TP),
            P(None, REP, TP),
            P(None, REP, TP),
            P(REP, None, None, TP),
            P(None, REP, TP),
            P(None, REP, TP),
            P(REP, None, TP, None),
            P(None, TP, REP),
            P(None, TP, REP),
        ),
        out_specs=(
            P(None, None, TP),
            P(None, REP, TP),
            P(None, REP, TP),
            P(None, None, TP),
            P(None, REP, TP),
            P(None, REP, TP),
            P(None, TP, None),
            P(None, TP, REP),
            P(None, TP, REP),
        ),
        check_vma=False,
    )
```

time: 192 us -> 79.4 us (0.41)
  blocking collectives: 79.9 us -> 0 us
  Pallas kernels: 0 us -> 61.8 us
  waiting for transfers between devices: 51.9 us -> 0 us
  starting transfers between devices: 14.4 us -> 0 us
  between operations: 14.2 us -> 0.67 us
  local copies, waits for them, and re-layouts: 25 us -> 16.7 us
  other arithmetic: 5.96 us -> 0 us
    all_to_all x3 -> x0, blocking collectives: 79.9 us -> none  [the longest x2 56.1 us: moved_by_axis(): out = lax.all_to_all(out, axes[k], k, k, tiled=True)]
    pallas_call x0 -> x1, Pallas kernels: none -> 61.8 us  [outer_step(): pl.pallas_call(outer_kernel, out_shape=tuple((pltpu.VMEM(*shape) for shap...]
    all_to_all x2 -> x0, waiting for transfers between devices: 51.9 us -> none  [the longest x1 28 us: outer_step(): lax.all_to_all(delta_output, REP, split_axis=3, concat_axis=0, tiled=True)]
    all_to_all x2 -> x0, starting transfers between devices: 14.3 us -> none  [the longest x1 9.58 us: outer_step(): lax.all_to_all(delta_output, REP, split_axis=3, concat_axis=0, tiled=True)]
    unnamed x22 -> x25, local copies, waits for them, and re-layouts: 20 us -> 16.7 us
    reduce_sum x3 -> x0, other arithmetic: 3.07 us -> none  [the longest x1 1.77 us: outer_step(): output_totals = jnp.sum(output_terms.astype(jnp.float32), 0)]
    convert_element_type x3 -> x0, other arithmetic: 2.89 us -> none  [the longest x1 1.1 us: outer_step(): output_master.astype(jnp.bfloat16)]
    reshape x1 -> x0, local copies, waits for them, and re-layouts: 2.39 us -> none  [moved_by_axis(): out = blocks.reshape(*(lax.axis_size(a) for a in axes), *inside)]
  transfers between devices with their start and end apart: 4 -> 0, of which waited for: 2 -> 0; matrix products, arithmetic and copies ran while one was open for 9% -> 0% of each run, Pallas kernels for 0% -> 0%
where the time goes in v1:
time: 79.4 us; the launch traced here: 79.1 us
  Pallas kernels  61.8 us (78%)
  local copies, waits for them, and re-layouts  16.7 us (21%)
    pallas_call x1, Pallas kernels, outer_step(): pl.pallas_call(outer_kernel, out_shape=tuple((pltpu.VMEM(*shape) for shap...  61.8 us
    unnamed x25, local copies, waits for them, and re-layouts  16.7 us

profile of v1, /device:TPU:1, one launch (start us, length us, event | category | flops | bytes accessed | tf_op | source)
XLA Modules:
  0.0 79.1 jit_solution(2777975084289783388)
XLA Ops:
  0.6 0.0 copy-start
  0.7 1.6 %copy-done = bf16[1,2,256,2048]{3,2,1,0:T(8,128)(2,1)S(1)} copy-done((bf16[1,2,256,2048]{3,2,1,0:T(8,128)(2,1)S(1)}, bf16[1,2,256,2048]{3,2,1,0:T(8,128)(2,1)}, u32[]{:S(2)}) %copy-start) | copy-done | bytes 2097176
  2.2 0.0 copy-start.1
  2.2 1.2 %copy-done.1 = bf16[1,2,512,512]{3,2,1,0:T(8,128)(2,1)S(1)} copy-done((bf16[1,2,512,512]{3,2,1,0:T(8,128)(2,1)S(1)}, bf16[1,2,512,512]{3,2,1,0:T(8,128)(2,1)}, u32[]{:S(2)}) %copy-start.1) | copy-done | bytes 1048600
  3.5 0.0 copy-start.2
  3.5 1.0 %copy-done.2 = f32[2,128,384]{2,1,0:T(8,128)S(1)} copy-done((f32[2,128,384]{2,1,0:T(8,128)S(1)}, f32[2,128,384]{2,1,0:T(8,128)}, u32[]{:S(2)}) %copy-start.2) | copy-done | bytes 393240
  4.5 0.0 copy-start.3
  4.5 1.0 %copy-done.3 = f32[2,128,384]{2,1,0:T(8,128)S(1)} copy-done((f32[2,128,384]{2,1,0:T(8,128)S(1)}, f32[2,128,384]{2,1,0:T(8,128)}, u32[]{:S(2)}) %copy-start.3) | copy-done | bytes 393240
  5.5 0.0 copy-start.4
  5.5 0.9 %copy-done.4 = f32[2,256,128]{2,1,0:T(8,128)S(1)} copy-done((f32[2,256,128]{2,1,0:T(8,128)S(1)}, f32[2,256,128]{2,1,0:T(8,128)}, u32[]{:S(2)}) %copy-start.4) | copy-done | bytes 262168
  6.4 0.0 copy-start.5
  6.4 0.9 %copy-done.5 = f32[2,256,128]{2,1,0:T(8,128)S(1)} copy-done((f32[2,256,128]{2,1,0:T(8,128)S(1)}, f32[2,256,128]{2,1,0:T(8,128)}, u32[]{:S(2)}) %copy-start.5) | copy-done | bytes 262168
  7.4 0.9 %copy-done.6 = f32[2,32,512]{2,1,0:T(8,128)S(1)} copy-done((f32[2,32,512]{2,1,0:T(8,128)S(1)}, f32[2,32,512]{2,1,0:T(8,128)}, u32[]{:S(2)}) %copy-start.6) | copy-done | bytes 131096
  8.3 0.9 %copy-done.7 = f32[2,32,512]{2,1,0:T(8,128)S(1)} copy-done((f32[2,32,512]{2,1,0:T(8,128)S(1)}, f32[2,32,512]{2,1,0:T(8,128)}, u32[]{:S(2)}) %copy-start.7) | copy-done | bytes 131096
  9.2 61.8 %shard_map.160 = (bf16[2,2,4,2,128,384]{5,4,3,2,1,0:T(8,128)(2,1)S(1)}, f32[2,128,384]{2,1,0:T(8,128)S(1)}, f32[2,128,384]{2,1,0:T(8,128)S(1)}, bf16[2,2,4,2,32,...) custom-call(bf16[2,2,4,2,128,384]{5,4,3,2,1,0:T(8,128)(2,1)} %bitcas, ...), custom_call_target="tpu_custom_call" | custom-call | tf_op jit(solution)/shard_map/pallas_call | solution.py:316
  70.9 1.7 %copy.27 = bf16[2,2048,384]{2,1,0:T(8,128)(2,1)} copy(bf16[2,2048,384]{2,1,0:T(8,128)(2,1)S(1)} %bitcast.5) | data formatting | bytes 6291456
  72.6 0.7 copy.31
  73.2 0.7 copy.32
  73.9 0.7 copy.34
  74.6 0.7 copy.35
  75.3 0.7 copy.28
  76.1 0.7 copy.29
  76.8 1.0 %copy.30 = bf16[2,512,512]{2,1,0:T(8,128)(2,1)} copy(bf16[2,512,512]{2,1,0:T(8,128)(2,1)S(1)} %bitcast.6) | data formatting | bytes 2097152
  77.8 1.3 %copy.33 = bf16[2,256,2048]{2,1,0:T(8,128)(2,1)} copy(bf16[2,256,2048]{2,1,0:T(8,128)(2,1)S(1)} %get-tuple-element.33) | data formatting | bytes 4194304
  (2 shorter events, 0.0 us)
Async XLA Ops:
  0.6 1.6 %copy-start = (bf16[1,2,256,2048]{3,2,1,0:T(8,128)(2,1)S(1)}, bf16[1,2,256,2048]{3,2,1,0:T(8,128)(2,1)}, u32[]{:S(2)}) copy-start(bf16[1,2,256,2048]{3,2,1,0:T(8,128)(2,1)} %param.15) | copy-start | bytes 6291460
  2.2 1.2 %copy-start.1 = (bf16[1,2,512,512]{3,2,1,0:T(8,128)(2,1)S(1)}, bf16[1,2,512,512]{3,2,1,0:T(8,128)(2,1)}, u32[]{:S(2)}) copy-start(bf16[1,2,512,512]{3,2,1,0:T(8,128)(2,1)} %param.12) | copy-start | bytes 3145732
  3.5 1.0 %copy-start.2 = (f32[2,128,384]{2,1,0:T(8,128)S(1)}, f32[2,128,384]{2,1,0:T(8,128)}, u32[]{:S(2)}) copy-start(f32[2,128,384]{2,1,0:T(8,128)} %refs_1_.1) | copy-start | bytes 1179652
  4.5 1.0 %copy-start.3 = (f32[2,128,384]{2,1,0:T(8,128)S(1)}, f32[2,128,384]{2,1,0:T(8,128)}, u32[]{:S(2)}) copy-start(f32[2,128,384]{2,1,0:T(8,128)} %refs_2_.1) | copy-start | bytes 1179652
  5.5 0.9 %copy-start.4 = (f32[2,256,128]{2,1,0:T(8,128)S(1)}, f32[2,256,128]{2,1,0:T(8,128)}, u32[]{:S(2)}) copy-start(f32[2,256,128]{2,1,0:T(8,128)} %refs_7_.1) | copy-start | bytes 786436
  6.4 0.9 %copy-start.5 = (f32[2,256,128]{2,1,0:T(8,128)S(1)}, f32[2,256,128]{2,1,0:T(8,128)}, u32[]{:S(2)}) copy-start(f32[2,256,128]{2,1,0:T(8,128)} %refs_8_.1) | copy-start | bytes 786436
  7.4 0.9 %copy-start.6 = (f32[2,32,512]{2,1,0:T(8,128)S(1)}, f32[2,32,512]{2,1,0:T(8,128)}, u32[]{:S(2)}) copy-start(f32[2,32,512]{2,1,0:T(8,128)} %refs_4_.1) | copy-start | bytes 393220
  8.3 0.9 %copy-start.7 = (f32[2,32,512]{2,1,0:T(8,128)S(1)}, f32[2,32,512]{2,1,0:T(8,128)}, u32[]{:S(2)}) copy-start(f32[2,32,512]{2,1,0:T(8,128)} %refs_5_.1) | copy-start | bytes 393220

commit v2 on v1

--- a/solution.py
+++ b/solution.py
@@ -292,6 +292,20 @@
         copy.wait_recv()
     for copy in started:
         copy.wait_send()
+
+
+def write_kernel(*refs):
+    sources, results, sem = refs[:9], refs[9:18], refs[18]
+    copies = []
+    for source, result in zip(sources, results):
+        for layer in range(LAYERS):
+            copies.append(
+                pltpu.make_async_copy(source.at[layer], result.at[layer], sem.at[len(copies)])
+            )
+    for copy in copies:
+        copy.start()
+    for copy in copies:
+        copy.wait()
 
 
 def outer_step(
@@ -313,10 +327,22 @@
     pieces = [(LAYERS, 4, 2), (LAYERS, 4, 2), (LAYERS, 2), (LAYERS, 2), (LAYERS, 2), (LAYERS, 4)]
     scratch = [pltpu.VMEM((*lead, *block), bf16) for lead in pieces for block in BLOCKS]
     scratch += [pltpu.VMEM((LAYERS, *block), f32) for _ in range(2) for block in BLOCKS]
+    operands = (
+        delta_query.reshape(shapes[0][0]),
+        master_query,
+        moment_query,
+        delta_latent.reshape(shapes[3][0]),
+        master_latent,
+        moment_latent,
+        delta_output.reshape(shapes[6][0]),
+        master_output,
+        moment_output,
+    )
+    operands = [pltpu.with_memory_space_constraint(x, pltpu.HBM) for x in operands]
     results = pl.pallas_call(
         outer_kernel,
         out_shape=tuple(pltpu.VMEM(*shape) for shape in shapes),
-        in_specs=[pl.BlockSpec(memory_space=pl.ANY)] * 9,
+        in_specs=[pl.BlockSpec(memory_space=pltpu.HBM)] * 9,
         out_specs=tuple(pl.BlockSpec(memory_space=pltpu.VMEM) for _ in range(9)),
         scratch_shapes=scratch
         + [
@@ -327,17 +353,16 @@
         compiler_params=pltpu.CompilerParams(
             collective_id=0, has_side_effects=True, vmem_limit_bytes=40 * 1024 * 1024
         ),
-    )(
-        delta_query.reshape(shapes[0][0]),
-        master_query,
-        moment_query,
-        delta_latent.reshape(shapes[3][0]),
-        master_latent,
-        moment_latent,
-        delta_output.reshape(shapes[6][0]),
-        master_output,
-        moment_output,
-    )
+    )(*operands)
+    results = [pltpu.with_memory_space_constraint(x, pltpu.VMEM) for x in results]
+    results = pl.pallas_call(
+        write_kernel,
+        out_shape=tuple(pltpu.HBM(*shape) for shape in shapes),
+        in_specs=[pl.BlockSpec(memory_space=pltpu.VMEM)] * 9,
+        out_specs=tuple(pl.BlockSpec(memory_space=pltpu.HBM) for _ in range(9)),
+        scratch_shapes=[pltpu.SemaphoreType.DMA((9 * LAYERS,))],
+        compiler_params=pltpu.CompilerParams(vmem_limit_bytes=4 * 1024 * 1024),
+    )(*results)
     query, latent = results[0], results[3]
     return (
         query.reshape(LAYERS, 2048, 384),

time: 79.4 us -> 64.1 us (0.81)
  local copies, waits for them, and re-layouts: 16.7 us -> 0 us
  Pallas kernels: 61.8 us -> 63.4 us
    unnamed x25 -> x0, local copies, waits for them, and re-layouts: 16.7 us -> none
    pallas_call x0 -> x1, Pallas kernels: none -> 3.27 us  [outer_step(): pl.pallas_call(write_kernel, out_shape=tuple((pltpu.HBM(*shape) for shape...]
    pallas_call x1, Pallas kernels: 61.8 us -> 60.1 us  [outer_step(): pl.pallas_call(outer_kernel, out_shape=tuple((pltpu.VMEM(*shape) for shap...]
where the time goes in v2:
time: 64.1 us; the launch traced here: 64 us
  Pallas kernels  63.4 us (99%)
  between operations  0.65 us (1%)
    pallas_call x1, Pallas kernels, outer_step(): pl.pallas_call(outer_kernel, out_shape=tuple((pltpu.VMEM(*shape) for shap...  60.1 us
    pallas_call x1, Pallas kernels, outer_step(): pl.pallas_call(write_kernel, out_shape=tuple((pltpu.HBM(*shape) for shape...  3.27 us

profile of v2, /device:TPU:1, one launch (start us, length us, event | category | flops | bytes accessed | tf_op | source)
XLA Modules:
  0.0 64.0 jit_solution(13334783240415574362)
XLA Ops:
  0.6 60.1 %shard_map.160 = (bf16[2,2,4,2,128,384]{5,4,3,2,1,0:T(8,128)(2,1)S(1)}, f32[2,128,384]{2,1,0:T(8,128)S(1)}, f32[2,128,384]{2,1,0:T(8,128)S(1)}, bf16[2,2,4,2,32,...) custom-call(bf16[2,2,4,2,128,384]{5,4,3,2,1,0:T(8,128)(2,1)} %bitcas, ...), custom_call_target="tpu_custom_call" | custom-call | tf_op jit(solution)/shard_map/pallas_call | solution.py:342
  60.7 3.3 %shard_map.161 = (bf16[2,2,4,2,128,384]{5,4,3,2,1,0:T(8,128)(2,1)}, f32[2,128,384]{2,1,0:T(8,128)}, f32[2,128,384]{2,1,0:T(8,128)}, bf16[2,2,4,2,32,512]{5,4,3,2...) custom-call(bf16[2,2,4,2,128,384]{5,4,3,2,1,0:T(8,128)(2,1)S(1)} %ge, ...), custom_call_target="tpu_custom_call" | custom-call | tf_op jit(solution)/shard_map/pallas_call | solution.py:358

commit v3 on v0

v3 whole, which is shorter than its diff:
```python
import math

import jax
import jax.numpy as jnp
from jax import lax
from jax.experimental import pallas as pl
from jax.experimental.pallas import tpu as pltpu
from jax.sharding import Mesh
from jax.sharding import PartitionSpec as P

REP = ("yh", "z", "c")
TP = ("yl", "x")
MESH = pl.DeviceIdType.MESH

OUTER_RATE = 0.7
OUTER_MOMENTUM = 0.9
REPLICAS = 16
LAYERS = 2

BLOCKS = ((128, 384), (32, 512), (256, 128))
PARTS = ((0, 0, 64), (0, 64, 64), (1, 0, 16), (1, 16, 16), (2, 0, 256))
A, B, C = (0,), (1, 2), (3, 4)
Z_FIRST, Y_FIRST = (A, B), (C,)
GROUPS = 56
SENDS = 4
LOADS = 4
SIZE_ROWS = 3 * 4096


def part_shape(p):
    array, _, rows = PARTS[p]
    return (rows, BLOCKS[array][1])


def outer_kernel(*refs):
    f32, bf16 = jnp.float32, jnp.bfloat16
    delta, master, moment = refs[0:9:3], refs[1:9:3], refs[2:9:3]
    params, new_master, new_moment = refs[9:18:3], refs[10:18:3], refs[11:18:3]
    n = len(PARTS)
    own, peer, far, direct, summed, across = (
        refs[18 + n * i : 18 + n * (i + 1)] for i in range(6)
    )
    rest = refs[18 + 6 * n :]
    held_master, held_moment = rest[0:3], rest[3:6]
    size, load_sem, send_sem, recv_sem = rest[6:]

    yh, z, c = (lax.axis_index(a) for a in REP)
    zs = [lax.rem(z + k, 4) for k in range(4)]
    ys = [yh, 1 - yh]
    core_to, y_to = {"c": 1 - c}, {"yh": 1 - yh}
    z_to = {1: {"z": zs[1]}, 3: {"z": zs[3]}}
    up, down = (1, 3), (3, 1)

    barrier = pltpu.get_barrier_semaphore()
    for to in (y_to, z_to[1], z_to[3], core_to):
        pl.semaphore_signal(barrier, inc=1, device_id=to, device_id_type=MESH)

    def wait_bytes(sem, total):
        piece = size.at[pl.ds(0, total // 256)]
        pltpu.make_async_remote_copy(
            src_ref=piece,
            dst_ref=piece,
            send_sem=sem,
            recv_sem=sem,
            device_id=core_to,
            device_id_type=MESH,
        ).wait_recv()

    groups, sent, load_bytes = {}, [0] * SENDS, [0] * LOADS

    def send(src, dst, to, group, which):
        index, total = groups.get(group, (len(groups), 0))
        count = 2 * math.prod(src.shape)
        groups[group] = (index, total + count)
        sent[which] += count
        pltpu.make_async_remote_copy(
            src_ref=src,
            dst_ref=dst,
            send_sem=send_sem.at[which],
            recv_sem=recv_sem.at[index],
            device_id=to,
            device_id_type=MESH,
        ).start()

    def arrive(*group):
        index, total = groups[group]
        wait_bytes(recv_sem.at[index], total)

    def load(src, dst, which, width):
        load_bytes[which] += width * math.prod(src.shape)
        pltpu.make_async_copy(src, dst, load_sem.at[which]).start()

    def block(ref, p, layer, y, zz, core):
        array, first, rows = PARTS[p]
        if array < 2:
            return ref[array].at[layer, y, zz, core, pl.ds(first, rows)]
        column = pl.multiple_of(((y * 4 + zz) * 2 + core) * 128, 128)
        return ref[2].at[layer, pl.ds(first, rows), pl.ds(column, 128)]

    both = slice(None)

    order = (
        (A, (2,), (0, 1), 0),
        (C, (2,), (1,), 1),
        (A, (1, 3), (0, 1), 2),
        (C, (1, 3), (1,), 2),
        (B, (2,), (0, 1), 2),
        (C, (0,), (1,), 2),
        (B, (1, 3), (0, 1), 2),
        (A, (0,), (0, 1), 2),
        (C, (2, 1, 3), (0,), 2),
        (B, (0,), (0, 1), 2),
        (C, (0,), (0,), 2),
    )
    for chunk, ks, js, which in order:
        for p in chunk:
            for k in ks:
                for j in js:
                    load(block(delta, p, both, ys[j], zs[k], c), own[p].at[:, k, j], which, 2)
    for a in range(3):
        load(master[a], held_master[a], 3, 4)
        load(moment[a], held_moment[a], 3, 4)

    pl.semaphore_wait(barrier, 4)

    for chunk, ks, js, which in order:
        for p in chunk:
            for k in ks:
                for j in js:
                    send(
                        block(delta, p, both, ys[j], zs[k], 1 - c),
                        peer[p].at[:, k, j],
                        core_to,
                        ("core", chunk, ks, js),
                        0,
                    )

    waited = set()

    def pair(step):
        chunk, ks, js, which = order[step]
        if which not in waited:
            waited.add(which)
            wait_bytes(load_sem.at[which], load_bytes[which])
        arrive("core", chunk, ks, js)
        for p in chunk:
            for k in ks:
                for j in js:
                    own[p][:, k, j] = own[p][:, k, j] + peer[p][:, k, j]

    def total_of(*pieces):
        return sum(piece.astype(f32) for piece in pieces)

    layers = range(LAYERS)

    def zy_far(chunk):
        for l in layers:
            for p in chunk:
                send(own[p].at[l, 2], far[p].at[l], z_to[up[l]], ("far", chunk), 1)

    def zy_direct(chunk):
        for l in layers:
            for p in chunk:
                k = down[l]
                send(own[p].at[l, k], direct[p].at[l], z_to[k], ("direct", chunk), 1)

    def zy_pass_on(chunk):
        arrive("far", chunk)
        for l in layers:
            for p in chunk:
                k = up[l]
                own[p][l, k] = total_of(own[p][l, k], far[p][l]).astype(bf16)
                send(own[p].at[l, k], summed[p].at[l], z_to[k], ("summed", chunk), 1)

    def zy_across(chunk):
        arrive("direct", chunk)
        arrive("summed", chunk)
        for p in chunk:
            for l in layers:
                own[p][l, 0, 1] = total_of(
                    own[p][l, 0, 1], direct[p][l, 1], summed[p][l, 1]
                ).astype(bf16)
            send(own[p].at[:, 0, 1], across[p].at[:, 0], y_to, ("y", chunk), 1)

    def yz_across(chunk, k):
        for p in chunk:
            send(own[p].at[:, k, 1], across[p].at[:, k], y_to, ("y", chunk, k), 1)

    def yz_far(chunk):
        arrive("y", chunk, 2)
        for l in layers:
            for p in chunk:
                own[p][l, 2, 0] = own[p][l, 2, 0] + across[p][l, 2]
                send(own[p].at[l, 2, 0], far[p].at[l, 0], z_to[up[l]], ("far", chunk), 1)

    def yz_direct(chunk):
        arrive("y", chunk, 1)
        arrive("y", chunk, 3)
        for l in layers:
            for p in chunk:
                k = down[l]
                own[p][l, k, 0] = own[p][l, k, 0] + across[p][l, k]
                send(own[p].at[l, k, 0], direct[p].at[l, 0], z_to[k], ("direct", chunk), 1)

    def yz_pass_on(chunk):
        arrive("far", chunk)
        for l in layers:
            for p in chunk:
                k = up[l]
                own[p][l, k, 0] = total_of(own[p][l, k, 0], across[p][l, k], far[p][l, 0]).astype(
                    bf16
                )
                send(own[p].at[l, k, 0], summed[p].at[l, 0], z_to[k], ("summed", chunk), 1)

    def update(chunk):
        for p in chunk:
            a, first, rows = PARTS[p]
            for l in layers:
                here = (l, pl.ds(first, rows))
                total = total_of(own[p][l, 0, 0], direct[p][l, 0], summed[p][l, 0], across[p][l, 0])
                average = total * (1.0 / REPLICAS)
                momentum = OUTER_MOMENTUM * held_moment[a][here] + average
                updated = held_master[a][here] - OUTER_RATE * (
                    average + OUTER_MOMENTUM * momentum
                )
                new_moment[a][here] = momentum
                new_master[a][here] = updated
                block(params, p, l, yh, z, c)[...] = updated.astype(bf16)

    def share(p, l, y, zz, to, group, which=2):
        piece = block(params, p, l, y, zz, c)
        send(piece, piece, to, group, which)

    def core_share(p, l, j, k):
        share(p, l, ys[j], zs[k], core_to, ("core",), 3)

    def gather_z(chunk, j):
        for name, way in (("up", up), ("down", down)):
            for l in layers:
                for p in chunk:
                    share(p, l, ys[j], z, z_to[way[l]], (name, chunk, j))

    def gather_own(chunk, j):
        for p in chunk:
            core_share(p, both, j, 0)

    def gather_y(chunk):
        for p in chunk:
            share(p, both, yh, z, y_to, ("across", chunk, "own"))

    def came(chunk, j, name):
        arrive(name, chunk, j)
        for l in layers:
            k = {"up": down[l], "down": up[l], "on": 2}[name]
            for p in chunk:
                if name == "up":
                    share(p, l, ys[j], zs[k], z_to[up[l]], ("on", chunk, j))
        for l in layers:
            k = {"up": down[l], "down": up[l], "on": 2}[name]
            for p in chunk:
                if chunk in Y_FIRST:
                    share(p, l, yh, zs[k], y_to, ("across", chunk, name))
                core_share(p, l, j, k)

    def came_across(chunk, name):
        arrive("across", chunk, name)
        for l in layers:
            k = {"own": 0, "up": down[l], "down": up[l], "on": 2}[name]
            for p in chunk:
                core_share(p, l, 1, k)

    pair(0)
    zy_far(A)
    pair(1)
    yz_across(C, 2)
    pair(2)
    zy_direct(A)
    pair(3)
    yz_across(C, 1)
    yz_across(C, 3)
    pair(4)
    zy_far(B)
    pair(5)
    yz_across(C, 0)
    pair(6)
    pair(7)
    pair(8)
    pair(9)
    pair(10)
    zy_pass_on(A)
    zy_direct(B)
    zy_pass_on(B)
    yz_far(C)
    zy_across(A)
    yz_direct(C)
    zy_across(B)
    yz_pass_on(C)
    wait_bytes(load_sem.at[3], load_bytes[3])
    arrive("y", A)
    update(A)
    gather_y(A)
    gather_z(A, 0)
    gather_own(A, 0)
    arrive("y", B)
    update(B)
    gather_y(B)
    arrive("y", C, 0)
    arrive("direct", C)
    arrive("summed", C)
    update(C)
    gather_z(C, 0)
    gather_y(C)
    gather_z(B, 0)
    gather_own(B, 0)
    gather_own(C, 0)
    came(A, 0, "up")
    came(A, 0, "down")
    came_across(A, "own")
    gather_z(A, 1)
    came(C, 0, "up")
    came(A, 0, "on")
    came(C, 0, "down")
    came_across(B, "own")
    gather_z(B, 1)
    came(C, 0, "on")
    came(B, 0, "up")
    came(B, 0, "down")
    came_across(C, "own")
    came(A, 1, "up")
    came(A, 1, "down")
    came_across(C, "up")
    came(B, 0, "on")
    came(B, 1, "up")
    came(A, 1, "on")
    came_across(C, "down")
    came(B, 1, "down")
    came(B, 1, "on")
    came_across(C, "on")
    arrive("core")
    for which in range(SENDS):
        wait_bytes(send_sem.at[which], sent[which])


def write_kernel(*refs):
    sources, results, sem = refs[:9], refs[9:18], refs[18]
    copies = []
    for source, result in zip(sources, results):
        for layer in range(LAYERS):
            copies.append(
                pltpu.make_async_copy(source.at[layer], result.at[layer], sem.at[len(copies)])
            )
    for copy in copies:
        copy.start()
    for copy in copies:
        copy.wait()


def outer_step(
    delta_query,
    master_query,
    moment_query,
    delta_latent,
    master_latent,
    moment_latent,
    delta_output,
    master_output,
    moment_output,
):
    f32, bf16 = jnp.float32, jnp.bfloat16
    shapes = []
    for a, block in enumerate(BLOCKS):
        whole = (LAYERS, 2, 4, 2, *block) if a < 2 else (LAYERS, block[0], 16 * block[1])
        shapes += [(whole, bf16), ((LAYERS, *block), f32), ((LAYERS, *block), f32)]
    z_first = {p for chunk in Z_FIRST for p in chunk}
    scratch = []
    for kind in range(6):
        for p in range(len(PARTS)):
            if kind < 2:
                lead = (LAYERS, 4, 2)
            elif kind < 5:
                lead = (LAYERS, 2 if p in z_first else 1)
            else:
                lead = (LAYERS, 1 if p in z_first else 4)
            scratch.append(pltpu.VMEM((*lead, *part_shape(p)), bf16))
    scratch += [pltpu.VMEM((LAYERS, *block), f32) for _ in range(2) for block in BLOCKS]
    operands = (
        delta_query.reshape(shapes[0][0]),
        master_query,
        moment_query,
        delta_latent.reshape(shapes[3][0]),
        master_latent,
        moment_latent,
        delta_output.reshape(shapes[6][0]),
        master_output,
        moment_output,
    )
    operands = [pltpu.with_memory_space_constraint(x, pltpu.HBM) for x in operands]
    results = pl.pallas_call(
        outer_kernel,
        out_shape=tuple(pltpu.VMEM(*shape) for shape in shapes),
        in_specs=[pl.BlockSpec(memory_space=pltpu.HBM)] * 9,
        out_specs=tuple(pl.BlockSpec(memory_space=pltpu.VMEM) for _ in range(9)),
        scratch_shapes=scratch
        + [
            pltpu.VMEM((SIZE_ROWS, 128), bf16),
            pltpu.SemaphoreType.DMA((LOADS,)),
            pltpu.SemaphoreType.DMA((SENDS,)),
            pltpu.SemaphoreType.DMA((GROUPS,)),
        ],
        compiler_params=pltpu.CompilerParams(
            collective_id=0, has_side_effects=True, vmem_limit_bytes=40 * 1024 * 1024
        ),
    )(*operands)
    results = [pltpu.with_memory_space_constraint(x, pltpu.VMEM) for x in results]
    results = pl.pallas_call(
        write_kernel,
        out_shape=tuple(pltpu.HBM(*shape) for shape in shapes),
        in_specs=[pl.BlockSpec(memory_space=pltpu.VMEM)] * 9,
        out_specs=tuple(pl.BlockSpec(memory_space=pltpu.HBM) for _ in range(9)),
        scratch_shapes=[pltpu.SemaphoreType.DMA((9 * LAYERS,))],
        compiler_params=pltpu.CompilerParams(vmem_limit_bytes=4 * 1024 * 1024),
    )(*results)
    query, latent = results[0], results[3]
    return (
        query.reshape(LAYERS, 2048, 384),
        *results[1:3],
        latent.reshape(LAYERS, 512, 512),
        *results[4:],
    )


def solution(mesh):
    torus = Mesh(mesh.devices.reshape(2, 4, 2, 2, 4), (*REP, *TP))
    return jax.shard_map(
        outer_step,
        mesh=torus,
        in_specs=(
            P(REP, None, None, TP),
            P(None, REP, TP),
            P(None, REP, TP),
            P(REP, None, None, TP),
            P(None, REP, TP),
            P(None, REP, TP),
            P(REP, None, TP, None),
            P(None, TP, REP),
            P(None, TP, REP),
        ),
        out_specs=(
            P(None, None, TP),
            P(None, REP, TP),
            P(None, REP, TP),
            P(None, None, TP),
            P(None, REP, TP),
            P(None, REP, TP),
            P(None, TP, None),
            P(None, TP, REP),
            P(None, TP, REP),
        ),
        check_vma=False,
    )
```

time: 192 us -> 60.3 us (0.31)
  blocking collectives: 79.9 us -> 0 us
  Pallas kernels: 0 us -> 59.5 us
  waiting for transfers between devices: 51.9 us -> 0 us
  local copies, waits for them, and re-layouts: 25 us -> 0 us
  starting transfers between devices: 14.4 us -> 0 us
  between operations: 14.2 us -> 0.65 us
  other arithmetic: 5.96 us -> 0 us
    all_to_all x3 -> x0, blocking collectives: 79.9 us -> none  [the longest x2 56.1 us: moved_by_axis(): out = lax.all_to_all(out, axes[k], k, k, tiled=True)]
    pallas_call x0 -> x2, Pallas kernels: none -> 59.5 us  [the longest x1 56.2 us: outer_step(): pl.pallas_call(outer_kernel, out_shape=tuple((pltpu.VMEM(*shape) for shap...]
    all_to_all x2 -> x0, waiting for transfers between devices: 51.9 us -> none  [the longest x1 28 us: outer_step(): lax.all_to_all(delta_output, REP, split_axis=3, concat_axis=0, tiled=True)]
    unnamed x22 -> x0, local copies, waits for them, and re-layouts: 20 us -> none
    all_to_all x2 -> x0, starting transfers between devices: 14.3 us -> none  [the longest x1 9.58 us: outer_step(): lax.all_to_all(delta_output, REP, split_axis=3, concat_axis=0, tiled=True)]
    reduce_sum x3 -> x0, other arithmetic: 3.07 us -> none  [the longest x1 1.77 us: outer_step(): output_totals = jnp.sum(output_terms.astype(jnp.float32), 0)]
    convert_element_type x3 -> x0, other arithmetic: 2.89 us -> none  [the longest x1 1.1 us: outer_step(): output_master.astype(jnp.bfloat16)]
    reshape x1 -> x0, local copies, waits for them, and re-layouts: 2.39 us -> none  [moved_by_axis(): out = blocks.reshape(*(lax.axis_size(a) for a in axes), *inside)]
  transfers between devices with their start and end apart: 4 -> 0, of which waited for: 2 -> 0; matrix products, arithmetic and copies ran while one was open for 9% -> 0% of each run, Pallas kernels for 0% -> 0%
where the time goes in v3:
time: 60.3 us; the launch traced here: 60.1 us
  Pallas kernels  59.5 us (99%)
  between operations  0.65 us (1%)
    pallas_call x1, Pallas kernels, outer_step(): pl.pallas_call(outer_kernel, out_shape=tuple((pltpu.VMEM(*shape) for shap...  56.2 us
    pallas_call x1, Pallas kernels, outer_step(): pl.pallas_call(write_kernel, out_shape=tuple((pltpu.HBM(*shape) for shape...  3.27 us

profile of v3, /device:TPU:1, one launch (start us, length us, event | category | flops | bytes accessed | tf_op | source)
XLA Modules:
  0.0 60.1 jit_solution(14489252864430344314)
XLA Ops:
  0.6 56.2 %shard_map.160 = (bf16[2,2,4,2,128,384]{5,4,3,2,1,0:T(8,128)(2,1)S(1)}, f32[2,128,384]{2,1,0:T(8,128)S(1)}, f32[2,128,384]{2,1,0:T(8,128)S(1)}, bf16[2,2,4,2,32,...) custom-call(bf16[2,2,4,2,128,384]{5,4,3,2,1,0:T(8,128)(2,1)} %bitcas, ...), custom_call_target="tpu_custom_call" | custom-call | tf_op jit(solution)/shard_map/pallas_call | solution.py:398
  56.9 3.3 %shard_map.161 = (bf16[2,2,4,2,128,384]{5,4,3,2,1,0:T(8,128)(2,1)}, f32[2,128,384]{2,1,0:T(8,128)}, f32[2,128,384]{2,1,0:T(8,128)}, bf16[2,2,4,2,32,512]{5,4,3,2...) custom-call(bf16[2,2,4,2,128,384]{5,4,3,2,1,0:T(8,128)(2,1)S(1)} %ge, ...), custom_call_target="tpu_custom_call" | custom-call | tf_op jit(solution)/shard_map/pallas_call | solution.py:415

commit v4 on v3

--- a/solution.py
+++ b/solution.py
@@ -27,6 +27,71 @@
 SIZE_ROWS = 3 * 4096
 
 
+SCHEDULE = (
+    ("pair", 0),
+    ("zy_far", A),
+    ("pair", 1),
+    ("yz_across", C, 2),
+    ("pair", 2),
+    ("zy_direct", A),
+    ("pair", 3),
+    ("yz_across", C, 1),
+    ("yz_across", C, 3),
+    ("pair", 4),
+    ("zy_far", B),
+    ("pair", 5),
+    ("yz_across", C, 0),
+    ("pair", 6),
+    ("pair", 7),
+    ("pair", 8),
+    ("pair", 9),
+    ("pair", 10),
+    ("zy_pass_on", A),
+    ("zy_direct", B),
+    ("zy_pass_on", B),
+    ("yz_far", C),
+    ("zy_across", A),
+    ("yz_direct", C),
+    ("zy_across", B),
+    ("yz_pass_on", C),
+    ("update", A),
+    ("gather_y", A),
+    ("gather_z", A, 0),
+    ("gather_own", A, 0),
+    ("update", B),
+    ("gather_y", B),
+    ("update", C),
+    ("gather_z", C, 0),
+    ("gather_y", C),
+    ("gather_z", B, 0),
+    ("gather_own", B, 0),
+    ("gather_own", C, 0),
+    ("came", A, 0, "up"),
+    ("came", A, 0, "down"),
+    ("came_across", A, "own"),
+    ("gather_z", A, 1),
+    ("came", C, 0, "up"),
+    ("came", A, 0, "on"),
+    ("came", C, 0, "down"),
+    ("came_across", B, "own"),
+    ("gather_z", B, 1),
+    ("came", C, 0, "on"),
+    ("came", B, 0, "up"),
+    ("came", B, 0, "down"),
+    ("came_across", C, "own"),
+    ("came", A, 1, "up"),
+    ("came", A, 1, "down"),
+    ("came_across", C, "up"),
+    ("came", B, 0, "on"),
+    ("came", B, 1, "up"),
+    ("came", A, 1, "on"),
+    ("came_across", C, "down"),
+    ("came", B, 1, "down"),
+    ("came", B, 1, "on"),
+    ("came_across", C, "on"),
+)
+
+
 def part_shape(p):
     array, _, rows = PARTS[p]
     return (rows, BLOCKS[array][1])
@@ -37,10 +102,9 @@
     delta, master, moment = refs[0:9:3], refs[1:9:3], refs[2:9:3]
     params, new_master, new_moment = refs[9:18:3], refs[10:18:3], refs[11:18:3]
     n = len(PARTS)
-    own, peer, far, direct, summed, across = (
-        refs[18 + n * i : 18 + n * (i + 1)] for i in range(6)
-    )
-    rest = refs[18 + 6 * n :]
+    own, give, peer = refs[18:21], refs[21:24], refs[24:27]
+    far, direct, summed, across = (refs[27 + n * i : 27 + n * (i + 1)] for i in range(4))
+    rest = refs[27 + 4 * n :]
     held_master, held_moment = rest[0:3], rest[3:6]
     size, load_sem, send_sem, recv_sem = rest[6:]
 
@@ -99,54 +163,62 @@
 
     both = slice(None)
 
-    order = (
-        (A, (2,), (0, 1), 0),
-        (C, (2,), (1,), 1),
-        (A, (1, 3), (0, 1), 2),
-        (C, (1, 3), (1,), 2),
-        (B, (2,), (0, 1), 2),
-        (C, (0,), (1,), 2),
-        (B, (1, 3), (0, 1), 2),
-        (A, (0,), (0, 1), 2),
-        (C, (2, 1, 3), (0,), 2),
-        (B, (0,), (0, 1), 2),
-        (C, (0,), (0,), 2),
-    )
-    for chunk, ks, js, which in order:
-        for p in chunk:
-            for k in ks:
-                for j in js:
-                    load(block(delta, p, both, ys[j], zs[k], c), own[p].at[:, k, j], which, 2)
+    def at(ref, p, l, k, y):
+        array, first, rows = PARTS[p]
+        return ref[array].at[l, k, y, pl.ds(first, rows)]
+
+    for k in (2, 1, 3, 0):
+        which = (2, 1, 0, 1)[k]
+        for mine, ref, core in ((False, give, 1 - c), (True, own, c)):
+            for a in range(3):
+                if a < 2:
+                    load(delta[a].at[:, :, zs[k], core], ref[a].at[:, k], which, 2)
+                else:
+                    for y in (0, 1):
+                        column = pl.multiple_of(((y * 4 + zs[k]) * 2 + core) * 128, 128)
+                        load(delta[a].at[:, :, pl.ds(column, 128)], ref[a].at[:, k, y], which, 2)
     for a in range(3):
         load(master[a], held_master[a], 3, 4)
         load(moment[a], held_moment[a], 3, 4)
 
     pl.semaphore_wait(barrier, 4)
 
-    for chunk, ks, js, which in order:
+    mate = ys[1]
+    order = (
+        (A, (2,), "both"),
+        (C, (2,), "mate"),
+        (A, (1, 3), "both"),
+        (C, (1, 3), "mate"),
+        (B, (2,), "both"),
+        (C, (0,), "mate"),
+        (B, (1, 3), "both"),
+        (A, (0,), "both"),
+        (C, (2, 1, 3), "mine"),
+        (B, (0,), "both"),
+        (C, (0,), "mine"),
+    )
+    place = {"both": both, "mate": mate, "mine": yh}
+    for step, (chunk, ks, y) in enumerate(order):
+        if step in (0, 2, 5):
+            which = (0, 2, 5).index(step)
+            wait_bytes(load_sem.at[which], load_bytes[which])
         for p in chunk:
             for k in ks:
-                for j in js:
-                    send(
-                        block(delta, p, both, ys[j], zs[k], 1 - c),
-                        peer[p].at[:, k, j],
-                        core_to,
-                        ("core", chunk, ks, js),
-                        0,
-                    )
-
-    waited = set()
+                send(
+                    at(give, p, both, k, place[y]),
+                    at(peer, p, both, k, place[y]),
+                    core_to,
+                    ("core", step),
+                    0,
+                )
 
     def pair(step):
-        chunk, ks, js, which = order[step]
-        if which not in waited:
-            waited.add(which)
-            wait_bytes(load_sem.at[which], load_bytes[which])
-        arrive("core", chunk, ks, js)
+        chunk, ks, y = order[step]
+        arrive("core", step)
         for p in chunk:
             for k in ks:
-                for j in js:
-                    own[p][:, k, j] = own[p][:, k, j] + peer[p][:, k, j]
+                total = at(own, p, both, k, place[y])
+                total[...] = total[...] + at(peer, p, both, k, place[y])[...]
 
     def total_of(*pieces):
         return sum(piece.astype(f32) for piece in pieces)
@@ -156,42 +228,45 @@
     def zy_far(chunk):
         for l in layers:
             for p in chunk:
-                send(own[p].at[l, 2], far[p].at[l], z_to[up[l]], ("far", chunk), 1)
+                send(at(own, p, l, 2, both), far[p].at[l], z_to[up[l]], ("far", chunk), 1)
 
     def zy_direct(chunk):
         for l in layers:
             for p in chunk:
                 k = down[l]
-                send(own[p].at[l, k], direct[p].at[l], z_to[k], ("direct", chunk), 1)
+                send(at(own, p, l, k, both), direct[p].at[l], z_to[k], ("direct", chunk), 1)
 
     def zy_pass_on(chunk):
         arrive("far", chunk)
         for l in layers:
             for p in chunk:
                 k = up[l]
-                own[p][l, k] = total_of(own[p][l, k], far[p][l]).astype(bf16)
-                send(own[p].at[l, k], summed[p].at[l], z_to[k], ("summed", chunk), 1)
+                total = at(own, p, l, k, both)
+                total[...] = total_of(total[...], far[p][l]).astype(bf16)
+                send(total, summed[p].at[l], z_to[k], ("summed", chunk), 1)
 
     def zy_across(chunk):
         arrive("direct", chunk)
         arrive("summed", chunk)
         for p in chunk:
             for l in layers:
-                own[p][l, 0, 1] = total_of(
-                    own[p][l, 0, 1], direct[p][l, 1], summed[p][l, 1]
-                ).astype(bf16)
-            send(own[p].at[:, 0, 1], across[p].at[:, 0], y_to, ("y", chunk), 1)
+                total = at(own, p, l, 0, mate)
+                total[...] = total_of(total[...], direct[p][l, mate], summed[p][l, mate]).astype(
+                    bf16
+                )
+            send(at(own, p, both, 0, mate), across[p].at[:, 0], y_to, ("y", chunk), 1)
 
     def yz_across(chunk, k):
         for p in chunk:
-            send(own[p].at[:, k, 1], across[p].at[:, k], y_to, ("y", chunk, k), 1)
+            send(at(own, p, both, k, mate), across[p].at[:, k], y_to, ("y", chunk, k), 1)
 
     def yz_far(chunk):
         arrive("y", chunk, 2)
         for l in layers:
             for p in chunk:
-                own[p][l, 2, 0] = own[p][l, 2, 0] + across[p][l, 2]
-                send(own[p].at[l, 2, 0], far[p].at[l, 0], z_to[up[l]], ("far", chunk), 1)
+                total = at(own, p, l, 2, yh)
+                total[...] = total[...] + across[p][l, 2]
+                send(total, far[p].at[l, 0], z_to[up[l]], ("far", chunk), 1)
 
     def yz_direct(chunk):
         arrive("y", chunk, 1)
@@ -199,25 +274,39 @@
         for l in layers:
             for p in chunk:
                 k = down[l]
-                own[p][l, k, 0] = own[p][l, k, 0] + across[p][l, k]
-                send(own[p].at[l, k, 0], direct[p].at[l, 0], z_to[k], ("direct", chunk), 1)
+                total = at(own, p, l, k, yh)
+                total[...] = total[...] + across[p][l, k]
+                send(total, direct[p].at[l, 0], z_to[k], ("direct", chunk), 1)
 
     def yz_pass_on(chunk):
         arrive("far", chunk)
         for l in layers:
             for p in chunk:
                 k = up[l]
-                own[p][l, k, 0] = total_of(own[p][l, k, 0], across[p][l, k], far[p][l, 0]).astype(
-                    bf16
-                )
-                send(own[p].at[l, k, 0], summed[p].at[l, 0], z_to[k], ("summed", chunk), 1)
+                total = at(own, p, l, k, yh)
+                total[...] = total_of(total[...], across[p][l, k], far[p][l, 0]).astype(bf16)
+                send(total, summed[p].at[l, 0], z_to[k], ("summed", chunk), 1)
+
+    state_here = []
 
     def update(chunk):
+        if not state_here:
+            wait_bytes(load_sem.at[3], load_bytes[3])
+            state_here.append(True)
+        if chunk in Z_FIRST:
+            arrive("y", chunk)
+        else:
+            arrive("y", chunk, 0)
+            arrive("direct", chunk)
+            arrive("summed", chunk)
         for p in chunk:
             a, first, rows = PARTS[p]
             for l in layers:
                 here = (l, pl.ds(first, rows))
-                total = total_of(own[p][l, 0, 0], direct[p][l, 0], summed[p][l, 0], across[p][l, 0])
+                j = yh if chunk in Z_FIRST else 0
+                total = total_of(
+                    at(own, p, l, 0, yh)[...], direct[p][l, j], summed[p][l, j], across[p][l, 0]
+                )
                 average = total * (1.0 / REPLICAS)
                 momentum = OUTER_MOMENTUM * held_moment[a][here] + average
                 updated = held_master[a][here] - OUTER_RATE * (
@@ -269,73 +358,25 @@
             for p in chunk:
                 core_share(p, l, 1, k)
 
-    pair(0)
-    zy_far(A)
-    pair(1)
-    yz_across(C, 2)
-    pair(2)
-    zy_direct(A)
-    pair(3)
-    yz_across(C, 1)
-    yz_across(C, 3)
-    pair(4)
-    zy_far(B)
-    pair(5)
-    yz_across(C, 0)
-    pair(6)
-    pair(7)
-    pair(8)
-    pair(9)
-    pair(10)
-    zy_pass_on(A)
-    zy_direct(B)
-    zy_pass_on(B)
-    yz_far(C)
-    zy_across(A)
-    yz_direct(C)
-    zy_across(B)
-    yz_pass_on(C)
-    wait_bytes(load_sem.at[3], load_bytes[3])
-    arrive("y", A)
-    update(A)
-    gather_y(A)
-    gather_z(A, 0)
-    gather_own(A, 0)
-    arrive("y", B)
-    update(B)
-    gather_y(B)
-    arrive("y", C, 0)
-    arrive("direct", C)
-    arrive("summed", C)
-    update(C)
-    gather_z(C, 0)
-    gather_y(C)
-    gather_z(B, 0)
-    gather_own(B, 0)
-    gather_own(C, 0)
-    came(A, 0, "up")
-    came(A, 0, "down")
-    came_across(A, "own")
-    gather_z(A, 1)
-    came(C, 0, "up")
-    came(A, 0, "on")
-    came(C, 0, "down")
-    came_across(B, "own")
-    gather_z(B, 1)
-    came(C, 0, "on")
-    came(B, 0, "up")
-    came(B, 0, "down")
-    came_across(C, "own")
-    came(A, 1, "up")
-    came(A, 1, "down")
-    came_across(C, "up")
-    came(B, 0, "on")
-    came(B, 1, "up")
-    came(A, 1, "on")
-    came_across(C, "down")
-    came(B, 1, "down")
-    came(B, 1, "on")
-    came_across(C, "on")
+    stages = dict(
+        pair=pair,
+        zy_far=zy_far,
+        zy_direct=zy_direct,
+        zy_pass_on=zy_pass_on,
+        zy_across=zy_across,
+        yz_across=yz_across,
+        yz_far=yz_far,
+        yz_direct=yz_direct,
+        yz_pass_on=yz_pass_on,
+        update=update,
+        gather_y=gather_y,
+        gather_z=gather_z,
+        gather_own=gather_own,
+        came=came,
+        came_across=came_across,
+    )
+    for name, *rest in SCHEDULE:
+        stages[name](*rest)
     arrive("core")
     for which in range(SENDS):
         wait_bytes(send_sem.at[which], sent[which])
@@ -373,11 +414,10 @@
         shapes += [(whole, bf16), ((LAYERS, *block), f32), ((LAYERS, *block), f32)]
     z_first = {p for chunk in Z_FIRST for p in chunk}
     scratch = []
-    for kind in range(6):
+    scratch += [pltpu.VMEM((LAYERS, 4, 2, *block), bf16) for _ in range(3) for block in BLOCKS]
+    for kind in range(4):
         for p in range(len(PARTS)):
-            if kind < 2:
-                lead = (LAYERS, 4, 2)
-            elif kind < 5:
+            if kind < 3:
                 lead = (LAYERS, 2 if p in z_first else 1)
             else:
                 lead = (LAYERS, 1 if p in z_first else 4)

time: 60.3 us -> 60 us (level)
  no operation moved by 1% of the time
where the time goes in v4:
time: 60 us; the launch traced here: 59.9 us
  Pallas kernels  59.3 us (99%)
  between operations  0.65 us (1%)
    pallas_call x1, Pallas kernels, outer_step(): pl.pallas_call(outer_kernel, out_shape=tuple((pltpu.VMEM(*shape) for shap...  56 us
    pallas_call x1, Pallas kernels, outer_step(): pl.pallas_call(write_kernel, out_shape=tuple((pltpu.HBM(*shape) for shape...  3.27 us

profile of v4, /device:TPU:1, one launch (start us, length us, event | category | flops | bytes accessed | tf_op | source)
XLA Modules:
  0.0 59.9 jit_solution(14476140076472558443)
XLA Ops:
  0.6 56.0 %shard_map.160 = (bf16[2,2,4,2,128,384]{5,4,3,2,1,0:T(8,128)(2,1)S(1)}, f32[2,128,384]{2,1,0:T(8,128)S(1)}, f32[2,128,384]{2,1,0:T(8,128)S(1)}, bf16[2,2,4,2,32,...) custom-call(bf16[2,2,4,2,128,384]{5,4,3,2,1,0:T(8,128)(2,1)} %bitcas, ...), custom_call_target="tpu_custom_call" | custom-call | tf_op jit(solution)/shard_map/pallas_call | solution.py:438
  56.7 3.3 %shard_map.161 = (bf16[2,2,4,2,128,384]{5,4,3,2,1,0:T(8,128)(2,1)}, f32[2,128,384]{2,1,0:T(8,128)}, f32[2,128,384]{2,1,0:T(8,128)}, bf16[2,2,4,2,32,512]{5,4,3,2...) custom-call(bf16[2,2,4,2,128,384]{5,4,3,2,1,0:T(8,128)(2,1)S(1)} %ge, ...), custom_call_target="tpu_custom_call" | custom-call | tf_op jit(solution)/shard_map/pallas_call | solution.py:455

commit v5 on v4

--- a/solution.py
+++ b/solution.py
@@ -18,10 +18,33 @@
 LAYERS = 2
 
 BLOCKS = ((128, 384), (32, 512), (256, 128))
-PARTS = ((0, 0, 64), (0, 64, 64), (1, 0, 16), (1, 16, 16), (2, 0, 256))
-A, B, C = (0,), (1, 2), (3, 4)
-Z_FIRST, Y_FIRST = (A, B), (C,)
-GROUPS = 56
+PARTS = (
+    (0, 0, 48),
+    (0, 48, 48),
+    (0, 96, 32),
+    (1, 0, 16),
+    (1, 16, 16),
+    (2, 0, 256),
+)
+A, B, C, D = (0,), (1,), (2, 3), (4, 5)
+Z_FIRST, Y_FIRST = (A, B, C,), (D,)
+ORDER = (
+    (A, (2,), "both"),
+    (D, (2,), "mate"),
+    (A, (1, 3), "both"),
+    (B, (2,), "both"),
+    (C, (2,), "both"),
+    (D, (1, 3), "mate"),
+    (B, (1, 3), "both"),
+    (C, (1, 3), "both"),
+    (D, (0,), "mate"),
+    (D, (2, 1, 3), "mine"),
+    (A, (0,), "both"),
+    (B, (0,), "both"),
+    (C, (0,), "both"),
+    (D, (0,), "mine"),
+)
+GROUPS = 62
 SENDS = 4
 LOADS = 4
 SIZE_ROWS = 3 * 4096
@@ -31,64 +54,83 @@
     ("pair", 0),
     ("zy_far", A),
     ("pair", 1),
-    ("yz_across", C, 2),
+    ("yz_across", D, 2),
+    ("pair", 4),
+    ("pair", 3),
+    ("zy_far", B),
+    ("pair", 5),
+    ("yz_across", D, 3),
+    ("pair", 6),
+    ("zy_far", C),
+    ("pair", 11),
+    ("pair", 12),
+    ("pair", 7),
+    ("pair", 8),
     ("pair", 2),
     ("zy_direct", A),
-    ("pair", 3),
-    ("yz_across", C, 1),
-    ("yz_across", C, 3),
-    ("pair", 4),
-    ("zy_far", B),
-    ("pair", 5),
-    ("yz_across", C, 0),
-    ("pair", 6),
-    ("pair", 7),
-    ("pair", 8),
+    ("yz_across", D, 1),
+    ("zy_pass_on", B),
+    ("zy_direct", B),
+    ("zy_pass_on", C),
+    ("yz_across", D, 0),
+    ("zy_direct", C),
+    ("pair", 10),
     ("pair", 9),
-    ("pair", 10),
+    ("yz_far", D),
     ("zy_pass_on", A),
-    ("zy_direct", B),
-    ("zy_pass_on", B),
-    ("yz_far", C),
-    ("zy_across", A),
-    ("yz_direct", C),
+    ("yz_direct", D),
     ("zy_across", B),
-    ("yz_pass_on", C),
-    ("update", A),
-    ("gather_y", A),
-    ("gather_z", A, 0),
-    ("gather_own", A, 0),
+    ("zy_across", C),
+    ("yz_pass_on", D),
+    ("pair", 13),
     ("update", B),
     ("gather_y", B),
+    ("gather_z", B, 0),
+    ("zy_across", A),
     ("update", C),
+    ("gather_y", C),
     ("gather_z", C, 0),
-    ("gather_y", C),
-    ("gather_z", B, 0),
-    ("gather_own", B, 0),
-    ("gather_own", C, 0),
-    ("came", A, 0, "up"),
-    ("came", A, 0, "down"),
+    ("update", D),
+    ("gather_own", D, 0),
+    ("gather_z", D, 0),
+    ("gather_y", D),
+    ("came", B, 0, "up"),
+    ("update", A),
+    ("gather_z", A, 0),
+    ("came_across", C, "own"),
+    ("gather_y", A),
+    ("came", C, 0, "up"),
+    ("came", D, 0, "up"),
+    ("came_across", B, "own"),
+    ("gather_z", B, 1),
+    ("came", B, 0, "down"),
+    ("came", D, 0, "down"),
     ("came_across", A, "own"),
     ("gather_z", A, 1),
-    ("came", C, 0, "up"),
+    ("came", D, 0, "on"),
+    ("gather_z", C, 1),
+    ("came", A, 0, "up"),
+    ("gather_own", C, 0),
+    ("came", A, 1, "up"),
+    ("came", B, 1, "up"),
+    ("came", A, 0, "down"),
+    ("came_across", D, "up"),
+    ("came", C, 1, "up"),
+    ("came_across", D, "own"),
+    ("came", B, 1, "down"),
+    ("came", C, 1, "down"),
+    ("came", A, 1, "down"),
+    ("came", B, 0, "on"),
+    ("came_across", D, "down"),
+    ("gather_own", B, 0),
+    ("gather_own", A, 0),
+    ("came", C, 0, "on"),
+    ("came", B, 1, "on"),
     ("came", A, 0, "on"),
+    ("came", A, 1, "on"),
     ("came", C, 0, "down"),
-    ("came_across", B, "own"),
-    ("gather_z", B, 1),
-    ("came", C, 0, "on"),
-    ("came", B, 0, "up"),
-    ("came", B, 0, "down"),
-    ("came_across", C, "own"),
-    ("came", A, 1, "up"),
-    ("came", A, 1, "down"),
-    ("came_across", C, "up"),
-    ("came", B, 0, "on"),
-    ("came", B, 1, "up"),
-    ("came", A, 1, "on"),
-    ("came_across", C, "down"),
-    ("came", B, 1, "down"),
-    ("came", B, 1, "on"),
-    ("came_across", C, "on"),
+    ("came_across", D, "on"),
+    ("came", C, 1, "on"),
 )
 
 
@@ -184,24 +226,14 @@
     pl.semaphore_wait(barrier, 4)
 
     mate = ys[1]
-    order = (
-        (A, (2,), "both"),
-        (C, (2,), "mate"),
-        (A, (1, 3), "both"),
-        (C, (1, 3), "mate"),
-        (B, (2,), "both"),
-        (C, (0,), "mate"),
-        (B, (1, 3), "both"),
-        (A, (0,), "both"),
-        (C, (2, 1, 3), "mine"),
-        (B, (0,), "both"),
-        (C, (0,), "mine"),
-    )
     place = {"both": both, "mate": mate, "mine": yh}
-    for step, (chunk, ks, y) in enumerate(order):
-        if step in (0, 2, 5):
-            which = (0, 2, 5).index(step)
-            wait_bytes(load_sem.at[which], load_bytes[which])
+    loaded = set()
+    for step, (chunk, ks, y) in enumerate(ORDER):
+        for k in ks:
+            which = (2, 1, 0, 1)[k]
+            if which not in loaded:
+                loaded.add(which)
+                wait_bytes(load_sem.at[which], load_bytes[which])
         for p in chunk:
             for k in ks:
                 send(
@@ -213,7 +245,7 @@
                 )
 
     def pair(step):
-        chunk, ks, y = order[step]
+        chunk, ks, y = ORDER[step]
         arrive("core", step)
         for p in chunk:
             for k in ks:

time: 60 us -> 56.1 us (0.935)
  Pallas kernels: 59.3 us -> 55.3 us
    pallas_call x1, Pallas kernels: 56 us -> 52 us  [outer_step(): pl.pallas_call(outer_kernel, out_shape=tuple((pltpu.VMEM(*shape) for shap...]
where the time goes in v5:
time: 56.1 us; the launch traced here: 55.9 us
  Pallas kernels  55.3 us (99%)
  between operations  0.65 us (1%)
    pallas_call x1, Pallas kernels, outer_step(): pl.pallas_call(outer_kernel, out_shape=tuple((pltpu.VMEM(*shape) for shap...  52 us
    pallas_call x1, Pallas kernels, outer_step(): pl.pallas_call(write_kernel, out_shape=tuple((pltpu.HBM(*shape) for shape...  3.27 us

profile of v5, /device:TPU:1, one launch (start us, length us, event | category | flops | bytes accessed | tf_op | source)
XLA Modules:
  0.0 55.9 jit_solution(15470867952504613344)
XLA Ops:
  0.6 52.0 %shard_map.160 = (bf16[2,2,4,2,128,384]{5,4,3,2,1,0:T(8,128)(2,1)S(1)}, f32[2,128,384]{2,1,0:T(8,128)S(1)}, f32[2,128,384]{2,1,0:T(8,128)S(1)}, bf16[2,2,4,2,32,...) custom-call(bf16[2,2,4,2,128,384]{5,4,3,2,1,0:T(8,128)(2,1)} %bitcas, ...), custom_call_target="tpu_custom_call" | custom-call | tf_op jit(solution)/shard_map/pallas_call | solution.py:470
  52.7 3.3 %shard_map.161 = (bf16[2,2,4,2,128,384]{5,4,3,2,1,0:T(8,128)(2,1)}, f32[2,128,384]{2,1,0:T(8,128)}, f32[2,128,384]{2,1,0:T(8,128)}, bf16[2,2,4,2,32,512]{5,4,3,2...) custom-call(bf16[2,2,4,2,128,384]{5,4,3,2,1,0:T(8,128)(2,1)S(1)} %ge, ...), custom_call_target="tpu_custom_call" | custom-call | tf_op jit(solution)/shard_map/pallas_call | solution.py:487

commit v6 on v5

--- a/solution.py
+++ b/solution.py
@@ -22,9 +22,9 @@
     (0, 0, 48),
     (0, 48, 48),
     (0, 96, 32),
-    (1, 0, 16),
-    (1, 16, 16),
-    (2, 0, 256),
+    (2, 0, 48),
+    (1, 0, 32),
+    (2, 48, 208),
 )
 A, B, C, D = (0,), (1,), (2, 3), (4, 5)
 Z_FIRST, Y_FIRST = (A, B, C,), (D,)
@@ -46,7 +46,7 @@
 )
 GROUPS = 62
 SENDS = 4
-LOADS = 4
+LOADS = 5
 SIZE_ROWS = 3 * 4096
 
 
@@ -55,80 +55,80 @@
     ("zy_far", A),
     ("pair", 1),
     ("yz_across", D, 2),
-    ("pair", 4),
+    ("pair", 2),
     ("pair", 3),
     ("zy_far", B),
+    ("pair", 6),
+    ("zy_direct", B),
     ("pair", 5),
     ("yz_across", D, 3),
-    ("pair", 6),
+    ("pair", 4),
+    ("pair", 11),
+    ("zy_direct", A),
+    ("zy_pass_on", A),
+    ("pair", 10),
+    ("yz_across", D, 1),
+    ("pair", 7),
+    ("zy_pass_on", B),
+    ("pair", 9),
     ("zy_far", C),
-    ("pair", 11),
+    ("zy_direct", C),
+    ("zy_across", A),
+    ("yz_far", D),
+    ("pair", 13),
     ("pair", 12),
-    ("pair", 7),
     ("pair", 8),
-    ("pair", 2),
-    ("zy_direct", A),
-    ("yz_across", D, 1),
-    ("zy_pass_on", B),
-    ("zy_direct", B),
+    ("zy_across", B),
     ("zy_pass_on", C),
     ("yz_across", D, 0),
-    ("zy_direct", C),
-    ("pair", 10),
-    ("pair", 9),
-    ("yz_far", D),
-    ("zy_pass_on", A),
     ("yz_direct", D),
-    ("zy_across", B),
+    ("update", A),
+    ("yz_pass_on", D),
+    ("gather_y", A),
+    ("gather_z", A, 0),
+    ("update", B),
+    ("gather_z", B, 0),
+    ("gather_y", B),
     ("zy_across", C),
-    ("yz_pass_on", D),
-    ("pair", 13),
-    ("update", B),
-    ("gather_y", B),
-    ("gather_z", B, 0),
-    ("zy_across", A),
+    ("update", D),
+    ("gather_y", D),
+    ("gather_z", D, 0),
+    ("came", B, 0, "up"),
+    ("came_across", A, "own"),
     ("update", C),
     ("gather_y", C),
+    ("came_across", B, "own"),
+    ("gather_own", C, 0),
+    ("gather_z", A, 1),
+    ("came", D, 0, "up"),
+    ("gather_z", B, 1),
+    ("came_across", C, "own"),
     ("gather_z", C, 0),
-    ("update", D),
     ("gather_own", D, 0),
-    ("gather_z", D, 0),
-    ("gather_y", D),
-    ("came", B, 0, "up"),
-    ("update", A),
-    ("gather_z", A, 0),
-    ("came_across", C, "own"),
-    ("gather_y", A),
+    ("gather_own", A, 0),
+    ("came", D, 0, "down"),
+    ("gather_z", C, 1),
+    ("came", B, 1, "up"),
+    ("came", D, 0, "on"),
+    ("came", A, 1, "up"),
+    ("gather_own", B, 0),
+    ("came", B, 0, "on"),
+    ("came", B, 0, "down"),
+    ("came", A, 0, "up"),
+    ("came", B, 1, "down"),
     ("came", C, 0, "up"),
-    ("came", D, 0, "up"),
-    ("came_across", B, "own"),
-    ("gather_z", B, 1),
-    ("came", B, 0, "down"),
-    ("came", D, 0, "down"),
-    ("came_across", A, "own"),
-    ("gather_z", A, 1),
-    ("came", D, 0, "on"),
-    ("gather_z", C, 1),
-    ("came", A, 0, "up"),
-    ("gather_own", C, 0),
-    ("came", A, 1, "up"),
-    ("came", B, 1, "up"),
+    ("came_across", D, "own"),
+    ("came", C, 0, "down"),
+    ("came", C, 1, "up"),
+    ("came", A, 1, "on"),
+    ("came", C, 1, "down"),
+    ("came", A, 0, "on"),
+    ("came", B, 1, "on"),
+    ("came_across", D, "up"),
+    ("came_across", D, "down"),
     ("came", A, 0, "down"),
-    ("came_across", D, "up"),
-    ("came", C, 1, "up"),
-    ("came_across", D, "own"),
-    ("came", B, 1, "down"),
-    ("came", C, 1, "down"),
     ("came", A, 1, "down"),
-    ("came", B, 0, "on"),
-    ("came_across", D, "down"),
-    ("gather_own", B, 0),
-    ("gather_own", A, 0),
     ("came", C, 0, "on"),
-    ("came", B, 1, "on"),
-    ("came", A, 0, "on"),
-    ("came", A, 1, "on"),
-    ("came", C, 0, "down"),
     ("came_across", D, "on"),
     ("came", C, 1, "on"),
 )
@@ -209,12 +209,19 @@
         array, first, rows = PARTS[p]
         return ref[array].at[l, k, y, pl.ds(first, rows)]
 
+    first = PARTS[A[0]][2]
+    top = pl.ds(0, first)
+    for ref, core in ((give, 1 - c), (own, c)):
+        load(delta[0].at[:, :, zs[2], core, top], ref[0].at[:, 2, :, top], 4, 2)
     for k in (2, 1, 3, 0):
         which = (2, 1, 0, 1)[k]
-        for mine, ref, core in ((False, give, 1 - c), (True, own, c)):
+        for ref, core in ((give, 1 - c), (own, c)):
             for a in range(3):
                 if a < 2:
-                    load(delta[a].at[:, :, zs[k], core], ref[a].at[:, k], which, 2)
+                    below = pl.ds(first, BLOCKS[a][0] - first) if k == 2 and a == 0 else both
+                    load(
+                        delta[a].at[:, :, zs[k], core, below], ref[a].at[:, k, :, below], which, 2
+                    )
                 else:
                     for y in (0, 1):
                         column = pl.multiple_of(((y * 4 + zs[k]) * 2 + core) * 128, 128)
@@ -230,7 +237,7 @@
     loaded = set()
     for step, (chunk, ks, y) in enumerate(ORDER):
         for k in ks:
-            which = (2, 1, 0, 1)[k]
+            which = (2, 1, 0, 1)[k] if step else 4
             if which not in loaded:
                 loaded.add(which)
                 wait_bytes(load_sem.at[which], load_bytes[which])

time: 56.1 us -> 55.7 us (level)
  no operation moved by 1% of the time
where the time goes in v6:
time: 55.7 us; the launch traced here: 55.6 us
  Pallas kernels  55 us (99%)
  between operations  0.65 us (1%)
    pallas_call x1, Pallas kernels, outer_step(): pl.pallas_call(outer_kernel, out_shape=tuple((pltpu.VMEM(*shape) for shap...  51.7 us
    pallas_call x1, Pallas kernels, outer_step(): pl.pallas_call(write_kernel, out_shape=tuple((pltpu.HBM(*shape) for shape...  3.27 us

profile of v6, /device:TPU:1, one launch (start us, length us, event | category | flops | bytes accessed | tf_op | source)
XLA Modules:
  0.0 55.6 jit_solution(10633957834022732973)
XLA Ops:
  0.6 51.7 %shard_map.160 = (bf16[2,2,4,2,128,384]{5,4,3,2,1,0:T(8,128)(2,1)S(1)}, f32[2,128,384]{2,1,0:T(8,128)S(1)}, f32[2,128,384]{2,1,0:T(8,128)S(1)}, bf16[2,2,4,2,32,...) custom-call(bf16[2,2,4,2,128,384]{5,4,3,2,1,0:T(8,128)(2,1)} %bitcas, ...), custom_call_target="tpu_custom_call" | custom-call | tf_op jit(solution)/shard_map/pallas_call | solution.py:477
  52.3 3.3 %shard_map.161 = (bf16[2,2,4,2,128,384]{5,4,3,2,1,0:T(8,128)(2,1)}, f32[2,128,384]{2,1,0:T(8,128)}, f32[2,128,384]{2,1,0:T(8,128)}, bf16[2,2,4,2,32,512]{5,4,3,2...) custom-call(bf16[2,2,4,2,128,384]{5,4,3,2,1,0:T(8,128)(2,1)S(1)} %ge, ...), custom_call_target="tpu_custom_call" | custom-call | tf_op jit(solution)/shard_map/pallas_call | solution.py:494

commit v7 on v6

--- a/solution.py
+++ b/solution.py
@@ -44,7 +44,8 @@
     (C, (0,), "both"),
     (D, (0,), "mine"),
 )
-GROUPS = 62
+LAST = 9
+GROUPS = 52
 SENDS = 4
 LOADS = 5
 SIZE_ROWS = 3 * 4096
@@ -247,13 +248,17 @@
                     at(give, p, both, k, place[y]),
                     at(peer, p, both, k, place[y]),
                     core_to,
-                    ("core", step),
+                    ("core", min(step, LAST)),
                     0,
                 )
 
+    paired = set()
+
     def pair(step):
         chunk, ks, y = ORDER[step]
-        arrive("core", step)
+        if min(step, LAST) not in paired:
+            paired.add(min(step, LAST))
+            arrive("core", min(step, LAST))
         for p in chunk:
             for k in ks:
                 total = at(own, p, both, k, place[y])
@@ -273,7 +278,7 @@
         for l in layers:
             for p in chunk:
                 k = down[l]
-                send(at(own, p, l, k, both), direct[p].at[l], z_to[k], ("direct", chunk), 1)
+                send(at(own, p, l, k, both), direct[p].at[l], z_to[k], ("final", chunk), 1)
 
     def zy_pass_on(chunk):
         arrive("far", chunk)
@@ -282,11 +287,10 @@
                 k = up[l]
                 total = at(own, p, l, k, both)
                 total[...] = total_of(total[...], far[p][l]).astype(bf16)
-                send(total, summed[p].at[l], z_to[k], ("summed", chunk), 1)
+                send(total, summed[p].at[l], z_to[k], ("final", chunk), 1)
 
     def zy_across(chunk):
-        arrive("direct", chunk)
-        arrive("summed", chunk)
+        arrive("final", chunk)
         for p in chunk:
             for l in layers:
                 total = at(own, p, l, 0, mate)
@@ -296,11 +300,12 @@
             send(at(own, p, both, 0, mate), across[p].at[:, 0], y_to, ("y", chunk), 1)
 
     def yz_across(chunk, k):
-        for p in chunk:
-            send(at(own, p, both, k, mate), across[p].at[:, k], y_to, ("y", chunk, k), 1)
+        group = {0: ("final", chunk), 2: ("far y", chunk)}.get(k, ("side y", chunk))
+        for p in chunk:
+            send(at(own, p, both, k, mate), across[p].at[:, k], y_to, group, 1)
 
     def yz_far(chunk):
-        arrive("y", chunk, 2)
+        arrive("far y", chunk)
         for l in layers:
             for p in chunk:
                 total = at(own, p, l, 2, yh)
@@ -308,14 +313,13 @@
                 send(total, far[p].at[l, 0], z_to[up[l]], ("far", chunk), 1)
 
     def yz_direct(chunk):
-        arrive("y", chunk, 1)
-        arrive("y", chunk, 3)
+        arrive("side y", chunk)
         for l in layers:
             for p in chunk:
                 k = down[l]
                 total = at(own, p, l, k, yh)
                 total[...] = total[...] + across[p][l, k]
-                send(total, direct[p].at[l, 0], z_to[k], ("direct", chunk), 1)
+                send(total, direct[p].at[l, 0], z_to[k], ("final", chunk), 1)
 
     def yz_pass_on(chunk):
         arrive("far", chunk)
@@ -324,7 +328,7 @@
                 k = up[l]
                 total = at(own, p, l, k, yh)
                 total[...] = total_of(total[...], across[p][l, k], far[p][l, 0]).astype(bf16)
-                send(total, summed[p].at[l, 0], z_to[k], ("summed", chunk), 1)
+                send(total, summed[p].at[l, 0], z_to[k], ("final", chunk), 1)
 
     state_here = []
 
@@ -335,9 +339,7 @@
         if chunk in Z_FIRST:
             arrive("y", chunk)
         else:
-            arrive("y", chunk, 0)
-            arrive("direct", chunk)
-            arrive("summed", chunk)
+            arrive("final", chunk)
         for p in chunk:
             a, first, rows = PARTS[p]
             for l in layers:

time: 55.7 us -> 55.6 us (level)
  no operation moved by 1% of the time
where the time goes in v7:
time: 55.6 us; the launch traced here: 55.5 us
  Pallas kernels  54.9 us (99%)
  between operations  0.65 us (1%)
    pallas_call x1, Pallas kernels, outer_step(): pl.pallas_call(outer_kernel, out_shape=tuple((pltpu.VMEM(*shape) for shap...  51.6 us
    pallas_call x1, Pallas kernels, outer_step(): pl.pallas_call(write_kernel, out_shape=tuple((pltpu.HBM(*shape) for shape...  3.27 us

profile of v7, /device:TPU:1, one launch (start us, length us, event | category | flops | bytes accessed | tf_op | source)
XLA Modules:
  0.0 55.5 jit_solution(7883259161685405098)
XLA Ops:
  0.6 51.6 %shard_map.160 = (bf16[2,2,4,2,128,384]{5,4,3,2,1,0:T(8,128)(2,1)S(1)}, f32[2,128,384]{2,1,0:T(8,128)S(1)}, f32[2,128,384]{2,1,0:T(8,128)S(1)}, bf16[2,2,4,2,32,...) custom-call(bf16[2,2,4,2,128,384]{5,4,3,2,1,0:T(8,128)(2,1)} %bitcas, ...), custom_call_target="tpu_custom_call" | custom-call | tf_op jit(solution)/shard_map/pallas_call | solution.py:479
  52.3 3.3 %shard_map.161 = (bf16[2,2,4,2,128,384]{5,4,3,2,1,0:T(8,128)(2,1)}, f32[2,128,384]{2,1,0:T(8,128)}, f32[2,128,384]{2,1,0:T(8,128)}, bf16[2,2,4,2,32,512]{5,4,3,2...) custom-call(bf16[2,2,4,2,128,384]{5,4,3,2,1,0:T(8,128)(2,1)S(1)} %ge, ...), custom_call_target="tpu_custom_call" | custom-call | tf_op jit(solution)/shard_map/pallas_call | solution.py:496

commit v8 on v7

--- a/solution.py
+++ b/solution.py
@@ -431,8 +431,8 @@
             copies.append(
                 pltpu.make_async_copy(source.at[layer], result.at[layer], sem.at[len(copies)])
             )
-    for copy in copies:
-        copy.start()
+    for i, copy in enumerate(copies):
+        copy.start(priority=i % 2)
     for copy in copies:
         copy.wait()
 

time: 55.6 us -> 55.6 us (level)
  no operation moved by 1% of the time
where the time goes in v8:
time: 55.6 us; the launch traced here: 55.5 us
  Pallas kernels  54.9 us (99%)
  between operations  0.65 us (1%)
    pallas_call x1, Pallas kernels, outer_step(): pl.pallas_call(outer_kernel, out_shape=tuple((pltpu.VMEM(*shape) for shap...  51.6 us
    pallas_call x1, Pallas kernels, outer_step(): pl.pallas_call(write_kernel, out_shape=tuple((pltpu.HBM(*shape) for shape...  3.27 us

profile of v8, /device:TPU:1, one launch (start us, length us, event | category | flops | bytes accessed | tf_op | source)
XLA Modules:
  0.0 55.5 jit_solution(3119009406980535683)
XLA Ops:
  0.6 51.6 %shard_map.160 = (bf16[2,2,4,2,128,384]{5,4,3,2,1,0:T(8,128)(2,1)S(1)}, f32[2,128,384]{2,1,0:T(8,128)S(1)}, f32[2,128,384]{2,1,0:T(8,128)S(1)}, bf16[2,2,4,2,32,...) custom-call(bf16[2,2,4,2,128,384]{5,4,3,2,1,0:T(8,128)(2,1)} %bitcas, ...), custom_call_target="tpu_custom_call" | custom-call | tf_op jit(solution)/shard_map/pallas_call | solution.py:479
  52.3 3.3 %shard_map.161 = (bf16[2,2,4,2,128,384]{5,4,3,2,1,0:T(8,128)(2,1)}, f32[2,128,384]{2,1,0:T(8,128)}, f32[2,128,384]{2,1,0:T(8,128)}, bf16[2,2,4,2,32,512]{5,4,3,2...) custom-call(bf16[2,2,4,2,128,384]{5,4,3,2,1,0:T(8,128)(2,1)S(1)} %ge, ...), custom_call_target="tpu_custom_call" | custom-call | tf_op jit(solution)/shard_map/pallas_call | solution.py:496
